TPU v7x, 32 devices: a whole 2x2x4 slice. The times are simulated.
32 devices in a mesh: tp: 32 (over z, y, x, core).
Axes of the slice: x: 2, y: 2, z: 4, core: 2. Of those that a mesh axis runs over, the one named last changes fastest.
Arguments:
- tok_ids: int32 [2, 512], replicated
- next_ids: int32 [2, 512], replicated
- seq_lens: int32 [512], replicated
- embed: bfloat16 [49152, 2048], P('tp')
- ln_gain: bfloat16 [2048], replicated
- w_in: bfloat16 [2048, 18688], P(None, 'tp')
- w_out: bfloat16 [10240, 2048], P('tp')
- final_gain: bfloat16 [2048], replicated
- k_cache: bfloat16 [512, 2048, 128], P('tp')
- v_cache: bfloat16 [512, 2048, 128], P('tp')
Outputs:
- output 1: float32 [2, 512], replicated
- output 2: bfloat16 [512, 2048, 128], P('tp')
- output 3: bfloat16 [512, 2048, 128], P('tp')
All inputs are finite; a program needn't handle non-finite values.
Results may differ from a plain program's by a relative error of at most 0.001.
Values are sent between devices in bfloat16 or wider.
A program may use at most 1 GiB of HBM per device.

v0:
```python
import jax
import jax.numpy as jnp
from jax import lax
from jax.sharding import PartitionSpec as P

ROPE_BASE = 10000.0
NORM_EPS = 1e-6


def layer_norm(values, gain_vec):
    centered = values.astype(jnp.float32)
    centered = centered - jnp.mean(centered, axis=-1, keepdims=True)
    variance = jnp.mean(jnp.square(centered), axis=-1, keepdims=True)
    scaled = centered * lax.rsqrt(variance + NORM_EPS) * gain_vec.astype(jnp.float32)
    return scaled.astype(jnp.bfloat16)


def rotary(vectors, positions):
    half_dim = vectors.shape[-1] // 2
    inv_freq = ROPE_BASE ** (-jnp.arange(half_dim, dtype=jnp.float32) / half_dim)
    angles = positions.astype(jnp.float32)[..., None] * inv_freq
    cosine = jnp.cos(angles)
    sine_val = jnp.sin(angles)
    first_half = vectors[..., :half_dim]
    second_half = vectors[..., half_dim:]
    return jnp.concatenate([first_half * cosine - second_half * sine_val, second_half * cosine + first_half * sine_val], axis=-1)


def solution(mesh):
    group_size = mesh.shape['tp']

    def device_fn(tok_ids, next_ids, seq_lens, embed_loc, ln_gain, w_in_loc, w_out_loc, final_gain, k_loc, v_loc):
        batch_size = tok_ids.shape[1]
        batch_dev = batch_size // group_size
        model_dim = embed_loc.shape[1]
        vocab_dev = embed_loc.shape[0]
        cache_len = k_loc.shape[1]
        head_dim = k_loc.shape[2]
        in_dev = w_in_loc.shape[1]
        out_dev = w_out_loc.shape[0]
        kv_dev = 2 * head_dim // group_size
        attn_dev = 2 * out_dev - in_dev + kv_dev
        ff_dev = out_dev - attn_dev
        qkv_dev = attn_dev + kv_dev
        attn_width = attn_dev * group_size
        num_heads = attn_width // head_dim
        dev_index = lax.axis_index('tp')
        vocab_start = dev_index * vocab_dev
        own_lens = lax.dynamic_slice_in_dim(seq_lens, dev_index * batch_dev, batch_dev)
        time_ids = jnp.arange(cache_len)
        step_logp = []
        for step_idx in range(tok_ids.shape[0]):
            local_ids = tok_ids[step_idx] - vocab_start
            tok_here = (local_ids >= 0) & (local_ids < vocab_dev)
            emb_rows = jnp.take(embed_loc, jnp.clip(local_ids, 0, vocab_dev - 1), axis=0)
            x_rows = lax.psum(jnp.where(tok_here[:, None], emb_rows, jnp.zeros_like(emb_rows)), 'tp')
            normed = layer_norm(x_rows, ln_gain)
            proj_out = jnp.dot(normed, w_in_loc, preferred_element_type=jnp.float32).astype(jnp.bfloat16)
            gate_proj = proj_out[:, qkv_dev:qkv_dev + ff_dev].astype(jnp.float32)
            up_proj = proj_out[:, qkv_dev + ff_dev:].astype(jnp.float32)
            mlp_act = (jax.nn.silu(gate_proj) * up_proj).astype(jnp.bfloat16)
            qkv_own = lax.all_to_all(proj_out[:, :qkv_dev], 'tp', 0, 1, tiled=True)
            positions = own_lens + step_idx
            queries = qkv_own[:, :attn_width].reshape(batch_dev, num_heads, head_dim).astype(jnp.float32)
            q_rot = (rotary(queries, positions[:, None]) * head_dim ** -0.5).astype(jnp.bfloat16)
            k_new = rotary(qkv_own[:, attn_width:attn_width + head_dim].astype(jnp.float32), positions).astype(jnp.bfloat16)
            v_new = qkv_own[:, attn_width + head_dim:]
            write_mask = time_ids[None, :, None] == positions[:, None, None]
            k_loc = jnp.where(write_mask, k_new[:, None, :], k_loc)
            v_loc = jnp.where(write_mask, v_new[:, None, :], v_loc)
            scores = jnp.einsum('bhd,btd->bht', q_rot, k_loc, preferred_element_type=jnp.float32)
            visible = time_ids[None, None, :] <= positions[:, None, None]
            attn_probs = jax.nn.softmax(jnp.where(visible, scores, -jnp.inf), axis=-1).astype(jnp.bfloat16)
            attn_out = jnp.einsum('bht,btd->bhd', attn_probs, v_loc, preferred_element_type=jnp.float32).astype(jnp.bfloat16)
            attn_cols = lax.all_to_all(attn_out.reshape(batch_dev, attn_width), 'tp', 1, 0, tiled=True)
            combined = jnp.concatenate([attn_cols, mlp_act], axis=1)
            part_out = jnp.dot(combined, w_out_loc, preferred_element_type=jnp.float32).astype(jnp.bfloat16)
            layer_out = lax.psum(part_out, 'tp')
            resid_sum = x_rows.astype(jnp.float32) + layer_out.astype(jnp.float32)
            final_normed = layer_norm(resid_sum, final_gain)
            logits = jnp.einsum('bd,vd->bv', final_normed, embed_loc, preferred_element_type=jnp.float32) * model_dim ** -0.5
            row_max = lax.pmax(jnp.max(logits, axis=1), 'tp')
            exp_sum = lax.psum(jnp.sum(jnp.exp(logits - row_max[:, None]), axis=1), 'tp')
            local_next = next_ids[step_idx] - vocab_start
            next_here = (local_next >= 0) & (local_next < vocab_dev)
            picked = jnp.take_along_axis(logits, jnp.clip(local_next, 0, vocab_dev - 1)[:, None], axis=1)[:, 0]
            target = lax.psum(jnp.where(next_here, picked, 0.0), 'tp')
            step_logp.append(target - row_max - jnp.log(exp_sum))
        return jnp.stack(step_logp), k_loc, v_loc

    cache_spec = P('tp', None, None)
    return jax.shard_map(device_fn, mesh=mesh, in_specs=(P(), P(), P(), P('tp', None), P(), P(None, 'tp'), P('tp', None), P(), cache_spec, cache_spec), out_specs=(P(), cache_spec, cache_spec), check_vma=False)
```

profile of v0, /device:TPU:0, one launch (start us, length us, event | category | flops | bytes accessed | tf_op | source)
XLA Modules:
  0.0 543.3 jit_solution(11301740219399712577)
XLA Ops:
  9.0 8.8 %gather_fusion = bf16[512,2048]{1,0:T(8,128)(2,1)} fusion(bf16[1536,2048]{1,0:T(8,128)(2,1)} %param.17, s32[1024]{0:T(1024)S(1)} %pad_clamp_fusion.1), kind=kCustom, calls=%fused_computation.clone | custom fusion | bytes 4196352 | tf_op jit(solution)/shard_map/jit(_take)/gather | solution.py:55
  17.8 8.8 %gather_fusion.2 = bf16[512,2048]{1,0:T(8,128)(2,1)} fusion(bf16[1536,2048]{1,0:T(8,128)(2,1)} %param.17, s32[1024]{0:T(1024)S(1)} %pad_clamp_fusion), kind=kCustom, calls=%fused_computation.2.clone | custom fusion | bytes 4196352 | tf_op jit(solution)/shard_map/jit(_take)/gather | solution.py:55
  26.6 3.4 select_select_fusion.1
  30.0 1.6 select_select_fusion
  33.3 143.4 %all-reduce.9.cloned.1.call-done = (bf16[512,2048]{1,0:T(8,128)(2,1)}, bf16[512,2048]{1,0:T(8,128)(2,1)}) async-done(((bf16[512,2048]{1,0:T(8,128)(2,1)}, bf16[512,2048]{1,0:T(8,128)(2,1)}), (bf16[512,2048]{1,0:T(8,128)(2,1)}, bf16[512,2048]{1,0:T(8,128)(2,1)})) %all-reduce.9.cloned.1.call-update) | async-done | bytes 4194320 | tf_op jit(solution)/shard_map/psum | solution.py:56
  176.7 2.1 convert_reduce_fusion.1
  179.6 1.6 fusion.44
  182.8 4.0 all-to-all-start
  186.8 2.1 convert_reduce_fusion
  189.7 1.6 fusion.41
  194.6 4.4 all-to-all-start.2
  199.3 7.7 %all-to-all-done.2 = bf16[32,16,72]{2,1,0:T(8,128)(2,1)S(1)} async-done(((bf16[32,16,72]{2,1,0:T(8,128)(2,1)}), bf16[32,16,72]{2,1,0:T(8,128)(2,1)S(1)}, u32[]{:S(2)}, u32[]{:S(2)}) %all-to-all-start.2) | async-done | bytes 73760 | tf_op jit(solution)/shard_map/all_to_all | solution.py:62
  207.7 10.4 %fusion.89 = (f32[16,16]{1,0:T(8,128)S(1)}, f32[16,16,2048]{2,1,0:T(8,128)}) fusion(bf16[16,2048,128]{2,1,0:T(8,128)(2,1)} %param.22, pred[16,2048]{1,0:T(8,128)(4,1)S(1)} %get-tuple-element.69, bf16[16,128]{1,0:T(8,128)(2,1)S(1)} %pad_maximum_fusion, pred[16,2048]{1,0:T(8,128)(4,1)S(1)} %get-tuple-element.70, f32[16,16,64]{2,1,0:T(8,128)S(1)} %get-tuple-element.22, ...), kind=kOutput, calls=%fused_computation.180 | convolution fusion | flops 140085248 | bytes 10687488 | tf_op jit(solution)/shard_map/sub | solution.py:73
  218.1 9.2 %fusion.47 = bf16[16,16,128]{2,1,0:T(8,128)(2,1)S(1)} fusion(bf16[16,2048,128]{2,1,0:T(8,128)(2,1)} %param.23, pred[16,2048]{1,0:T(8,128)(4,1)S(1)} %get-tuple-element.69, bf16[16,128]{1,0:T(8,128)(2,1)S(1)} %get-tuple-element.26, f32[16,16,2048]{2,1,0:T(8,128)} %get-tuple-element.62, f32[16,16]{1,0:T(8,128)S(1)} %get-tuple-element.61), kind=kOutput, calls=%fused_computation.70 | convolution fusion | flops 139493376 | bytes 10589184 | tf_op jit(solution)/shard_map/bht,btd->bhd/dot_general | solution.py:74
  228.3 2.6 all-to-all-start.1
  231.1 13.9 %broadcast_select_fusion.1 = (bf16[16,2048,128]{2,1,0:T(8,128)(2,1)}, bf16[16,2048,128]{2,1,0:T(8,128)(2,1)}) fusion(pred[16,2048]{1,0:T(8,128)(4,1)S(1)} %get-tuple-element.56, bf16[16,2048,128]{2,1,0:T(8,128)(2,1)} %param.22, pred[16,2048]{1,0:T(8,128)(4,1)S(1)} %get-tuple-element.69, bf16[16,128]{1,0:T(8,128)(2,1)S(1)} %pad_maximum_fusion.1, ...), kind=kLoop, calls=%fused_computation.7 | loop fusion | flops 16777216 | bytes 33636352 | tf_op jit(solution)/shard_map/jit(_where)/select_n | solution.py:69
  245.0 5.1 fusion.88
  250.1 4.7 convolution_convert_fusion.2
  255.7 5.8 %all-to-all-start.3 = ((bf16[32,2,512]{2,1,0:T(2,128)(2,1)}), bf16[32,2,512]{2,1,0:T(2,128)(2,1)S(1)}, u32[]{:S(2)}, u32[]{:S(2)}) async-start(bf16[32,2,512]{2,1,0:T(2,128)(2,1)} %reshape.494), calls=%async_computation.3 | async-start | bytes 131072 | tf_op jit(solution)/shard_map/all_to_all | solution.py:75
  262.2 6.5 %all-to-all-done.3 = bf16[32,2,512]{2,1,0:T(2,128)(2,1)S(1)} async-done(((bf16[32,2,512]{2,1,0:T(2,128)(2,1)}), bf16[32,2,512]{2,1,0:T(2,128)(2,1)S(1)}, u32[]{:S(2)}, u32[]{:S(2)}) %all-to-all-start.3) | async-done | bytes 65568 | tf_op jit(solution)/shard_map/all_to_all | solution.py:75
  269.0 3.9 convolution_convert_fusion.1
  272.9 2.7 convolution_convert_fusion
  276.3 138.3 %all-reduce.7.cloned.1.call-done = (bf16[512,2048]{1,0:T(8,128)(2,1)}, bf16[512,2048]{1,0:T(8,128)(2,1)}) async-done(((bf16[512,2048]{1,0:T(8,128)(2,1)}, bf16[512,2048]{1,0:T(8,128)(2,1)}), (bf16[512,2048]{1,0:T(8,128)(2,1)}, bf16[512,2048]{1,0:T(8,128)(2,1)})) %all-reduce.7.cloned.1.call-update) | async-done | bytes 4194320 | tf_op jit(solution)/shard_map/psum | solution.py:78
  414.7 2.4 fusion.17
  418.0 8.0 %fusion.91 = (f32[512]{0:T(512)S(1)}, f32[512,1536]{1,0:T(8,128)}) fusion(bf16[1536,2048]{1,0:T(8,128)(2,1)} %param.17, bf16[512,2048]{1,0:T(8,128)(2,1)S(1)} %copy-done.9, bf16[512,2048]{1,0:T(8,128)(2,1)S(1)} %copy-done.5, f32[2048]{0:T(1024)S(1)} %convert_element_type.136, f32[512]{0:T(512)S(1)} %add_rsqrt_fusion.2, f32[512]{0:T(512)S(1)} %broadcast_multiply_fusion.2), kind=kOutput, calls=%fused_computation.182 | convolution fusion | flops 3230137856 | bytes 13645824 | tf_op jit(solution)/shard_map/bd,vd->bv/dot_general | solution.py:81
  425.9 8.5 %gather_fusion.1 = f32[512]{0:T(512)S(1)} fusion(f32[512,1536]{1,0:T(8,128)} %get-tuple-element.66, s32[512]{0:T(512)S(1)} %bitcast.53), kind=kCustom, calls=%fused_computation.1.clone | custom fusion | bytes 8192 | tf_op jit(solution)/shard_map/jit(take_along_axis)/gather | solution.py:86
  434.5 2.4 fusion.19
  437.8 7.9 %fusion.90 = (f32[512]{0:T(512)S(1)}, f32[512,1536]{1,0:T(8,128)}) fusion(bf16[1536,2048]{1,0:T(8,128)(2,1)} %param.17, bf16[512,2048]{1,0:T(8,128)(2,1)S(1)} %copy-done.8, bf16[512,2048]{1,0:T(8,128)(2,1)S(1)} %copy-done.3, f32[512]{0:T(512)S(1)} %add_rsqrt_fusion, f32[512]{0:T(512)S(1)} %broadcast_multiply_fusion, f32[2048]{0:T(1024)S(1)} %convert_element_type.136), kind=kOutput, calls=%fused_computation.181 | convolution fusion | flops 3230137856 | bytes 13645824 | tf_op jit(solution)/shard_map/bd,vd->bv/dot_general | solution.py:81
  445.7 38.6 %all-reduce.1 = (f32[512]{0:T(512)S(1)}, f32[512]{0:T(512)S(1)}) all-reduce(f32[512]{0:T(512)S(1)} %get-tuple-element.63, f32[512]{0:T(512)S(1)} %get-tuple-element.65), channel_id=1, replica_groups=mesh['tp'=32] {'tp'}, use_global_device_ids=true, to_apply=%region_23.26 | all-reduce | flops 1024 | bytes 8192 | tf_op jit(solution)/shard_map/pmax | solution.py:82
  484.3 2.6 exponential_reduce_fusion.1
  487.7 8.8 %gather_fusion.3 = f32[512]{0:T(512)S(1)} fusion(f32[512,1536]{1,0:T(8,128)} %get-tuple-element.64, s32[512]{0:T(512)S(1)} %bitcast.52), kind=kCustom, calls=%fused_computation.3.clone | custom fusion | bytes 8192 | tf_op jit(solution)/shard_map/jit(take_along_axis)/gather | solution.py:86
  496.5 39.3 %all-reduce = (f32[512]{0:T(512)S(1)}, f32[512]{0:T(512)S(1)}, f32[512]{0:T(512)S(1)}, f32[512]{0:T(512)S(1)}) all-reduce(f32[512]{0:T(512)S(1)} %exponential_reduce_fusion, f32[512]{0:T(512)S(1)} %broadcast_select_fusion.10, f32[512]{0:T(512)S(1)} %exponential_reduce_fusion.1, ...), channel_id=1, replica_groups=mesh['tp'=32] {'tp'}, use_global_device_ids=true, to_apply=%region_25.28 | all-reduce | flops 2048 | bytes 16384 | tf_op jit(solution)/shard_map/psum | solution.py:83
  (105 shorter events, 17.7 us)
Async XLA Ops:
  7.2 172.4 %copy-start = (bf16[2048,584]{0,1:T(8,128)(2,1)S(1)}, bf16[2048,584]{0,1:T(8,128)(2,1)}, u32[]{:S(2)}) copy-start(bf16[2048,584]{0,1:T(8,128)(2,1)} %param.19) | copy-start | bytes 7176196
  7.2 169.5 %all-reduce.9.cloned.1.call-start = ((), (), s32[]{:S(2)}) async-start(), calls=%async_computation.5 | async-start | bytes 8388608 | tf_op jit(solution)/shard_map/psum | solution.py:56
  26.6 3.4 copy-start.7
  31.7 0.7 copy-start.12
  176.7 2.2 copy-start.4
  181.2 0.8 copy-start.10
  182.8 11.8 %all-to-all-start = ((bf16[32,16,72]{2,1,0:T(8,128)(2,1)}), bf16[32,16,72]{2,1,0:T(8,128)(2,1)S(1)}, u32[]{:S(2)}, u32[]{:S(2)}) async-start(bf16[32,16,72]{2,1,0:T(8,128)(2,1)} %bitcast.2), calls=%async_computation | async-start | bytes 262144 | tf_op jit(solution)/shard_map/all_to_all | solution.py:62
  186.8 2.2 copy-start.2
  194.6 12.4 %all-to-all-start.2 = ((bf16[32,16,72]{2,1,0:T(8,128)(2,1)}), bf16[32,16,72]{2,1,0:T(8,128)(2,1)S(1)}, u32[]{:S(2)}, u32[]{:S(2)}) async-start(bf16[32,16,72]{2,1,0:T(8,128)(2,1)} %bitcast.14), calls=%async_computation.2 | async-start | bytes 262144 | tf_op jit(solution)/shard_map/all_to_all | solution.py:62
  228.3 27.4 %all-to-all-start.1 = ((bf16[32,2,512]{2,1,0:T(2,128)(2,1)}), bf16[32,2,512]{2,1,0:T(2,128)(2,1)S(1)}, u32[]{:S(2)}, u32[]{:S(2)}) async-start(bf16[32,2,512]{2,1,0:T(2,128)(2,1)} %reshape.496), calls=%async_computation.1 | async-start | bytes 131072 | tf_op jit(solution)/shard_map/all_to_all | solution.py:75
  255.7 13.0 %all-to-all-start.3 = ((bf16[32,2,512]{2,1,0:T(2,128)(2,1)}), bf16[32,2,512]{2,1,0:T(2,128)(2,1)S(1)}, u32[]{:S(2)}, u32[]{:S(2)}) async-start(bf16[32,2,512]{2,1,0:T(2,128)(2,1)} %reshape.494), calls=%async_computation.3 | async-start | bytes 131072 | tf_op jit(solution)/shard_map/all_to_all | solution.py:75
  261.5 153.2 %all-reduce.7.cloned.1.call-start = ((), (), s32[]{:S(2)}) async-start(), calls=%async_computation.4 | async-start | bytes 8388608 | tf_op jit(solution)/shard_map/psum | solution.py:78
  262.2 10.6 %copy-start.14 = (bf16[320,2048]{1,0:T(8,128)(2,1)S(1)}, bf16[320,2048]{1,0:T(8,128)(2,1)}, u32[]{:S(2)}) copy-start(bf16[320,2048]{1,0:T(8,128)(2,1)} %param.20) | copy-start | bytes 3932164
  275.6 0.7 copy-start.13
  275.6 0.7 copy-start.11
  275.6 139.1 %copy-start.5 = (bf16[512,2048]{1,0:T(8,128)(2,1)S(1)}, bf16[512,2048]{1,0:T(8,128)(2,1)}, u32[]{:S(2)}) copy-start(bf16[512,2048]{1,0:T(8,128)(2,1)} %get-tuple-element.18) | copy-start | bytes 6291460
  414.7 2.4 copy-start.9
  425.9 8.5 %copy-start.3 = (bf16[512,2048]{1,0:T(8,128)(2,1)S(1)}, bf16[512,2048]{1,0:T(8,128)(2,1)}, u32[]{:S(2)}) copy-start(bf16[512,2048]{1,0:T(8,128)(2,1)} %get-tuple-element.17) | copy-start | bytes 6291460
  434.4 2.4 copy-start.8
  484.3 2.8 copy-start.6
  484.3 52.2 %copy-start.1 = (bf16[2048,584]{0,1:T(8,128)(2,1)S(1)}, bf16[2048,584]{0,1:T(8,128)(2,1)}, u32[]{:S(2)}) copy-start(bf16[2048,584]{0,1:T(8,128)(2,1)} %param.19) | copy-start | bytes 7176196
Sparse Core Ops, SparseCore 0:
  31.8 144.8 all-reduce.8
  275.7 138.9 all-reduce.6
where the time goes:
time: 545 us; the launch traced here: 543 us
  waiting for transfers between devices  297 us (54%)
  blocking collectives  77.9 us (14%)
  matrix products  55.1 us (10%)
  local copies, waits for them, and re-layouts  42 us (8%)
  other arithmetic  39.5 us (7%)
  starting transfers between devices  17.1 us (3%)
  between operations  14.5 us (3%)
    psum x1, waiting for transfers between devices, device_fn(): lax.psum(jnp.where(tok_here[:, None], emb_rows, jnp.zeros_like(emb_rows))...  143 us
    psum x1, waiting for transfers between devices, device_fn(): layer_out = lax.psum(part_out, 'tp')  138 us
    psum x1, blocking collectives, device_fn(): lax.psum(jnp.sum(jnp.exp(logits - row_max[:, None]), axis=1), 'tp')  39.3 us
    pmax x1, blocking collectives, device_fn(): row_max = lax.pmax(jnp.max(logits, axis=1), 'tp')  38.6 us
    gather x2, local copies, waits for them, and re-layouts, device_fn(): jnp.take(embed_loc, jnp.clip(local_ids, 0, vocab_dev - 1), axis=0)  17.6 us
    gather x2, local copies, waits for them, and re-layouts, device_fn(): jnp.take_along_axis(logits, jnp.clip(local_next, 0, vocab_dev - 1)[:, Non...  17.3 us
    dot_general x2, matrix products, device_fn(): jnp.einsum('bd,vd->bv', final_normed, embed_loc, preferred_element_type=j...  15.9 us
    sub x2, matrix products, device_fn(): jax.nn.softmax(jnp.where(visible, scores, -jnp.inf), axis=-1)  15.5 us
  transfers between devices with their start and end apart: 6, of which 5 were waited for; matrix products, arithmetic and copies ran while one was open for 6% of the time, Pallas kernels for 0%

commit v1 on v0

v1 whole, which is shorter than its diff:
```python
import functools

import jax
import jax.numpy as jnp
from jax import lax
from jax.experimental import pallas as pl
from jax.experimental.pallas import tpu as pltpu
from jax.sharding import PartitionSpec as P

ROPE_BASE = 10000.0
NORM_EPS = 1e-6
MESH_ID = pl.DeviceIdType.MESH
ROWS = 16
NZ = 4
NDEV = 32
STEPS = 2
RS_SPLIT = 2
AG_SPLIT = 1
BF16 = jnp.bfloat16
F32 = jnp.float32


def rotary(vectors, positions):
    half_dim = vectors.shape[-1] // 2
    inv_freq = ROPE_BASE ** (-jnp.arange(half_dim, dtype=jnp.float32) / half_dim)
    angles = positions.astype(jnp.float32)[..., None] * inv_freq
    cosine = jnp.cos(angles)
    sine_val = jnp.sin(angles)
    first_half = vectors[..., :half_dim]
    second_half = vectors[..., half_dim:]
    return jnp.concatenate([first_half * cosine - second_half * sine_val, second_half * cosine + first_half * sine_val], axis=-1)


def norm_rows(values, gain):
    centered = values - jnp.mean(values, axis=-1, keepdims=True)
    variance = jnp.mean(jnp.square(centered), axis=-1, keepdims=True)
    return (centered * lax.rsqrt(variance + NORM_EPS) * gain).astype(BF16)


def dot_nt(a, b):
    return lax.dot_general(a, b, (((1,), (1,)), ((), ())), preferred_element_type=F32)


class Place:
    def __init__(self):
        self.me = lax.axis_index("tp")
        self.c = lax.rem(self.me, 2)
        self.x = lax.rem(lax.div(self.me, 2), 2)
        self.y = lax.rem(lax.div(self.me, 4), 2)
        self.z = lax.div(self.me, 8)
        self.sib = self.me + 1 - 2 * self.c
        self.xpeer = self.me + 2 * (1 - 2 * self.x)
        self.ypeer = self.me + 4 * (1 - 2 * self.y)

    def zpeer(self, k):
        return lax.rem(self.me + 8 * k, NDEV)

    def peer(self, k):
        return lax.rem(self.me + k, NDEV)


def remote(src, dst, ssem, rsem, dev):
    return pltpu.make_async_remote_copy(src_ref=src, dst_ref=dst, send_sem=ssem, recv_sem=rsem, device_id=(dev,), device_id_type=MESH_ID)


def greet(place):
    barrier = pltpu.get_barrier_semaphore()

    def body(k, _):
        pl.semaphore_signal(barrier, inc=1, device_id=(place.peer(k),), device_id_type=MESH_ID)
        return 0

    lax.fori_loop(1, NDEV, body, 0)
    return barrier


def exchange_scratch(width):
    w = width // RS_SPLIT
    return dict(
        part=pltpu.VMEM((STEPS, NZ, 2, 2, 2, ROWS, width), BF16),
        rc=pltpu.VMEM((STEPS, NZ, 2, 2, ROWS, width), BF16),
        s1=pltpu.VMEM((STEPS, NZ, 2, 2, ROWS, width), BF16),
        r1a=pltpu.VMEM((STEPS, RS_SPLIT, NZ, 2, ROWS, w // 2), BF16),
        r1b=pltpu.VMEM((STEPS, RS_SPLIT, NZ, 2, ROWS, w // 2), BF16),
        s2a=pltpu.VMEM((STEPS, RS_SPLIT, NZ, 2, ROWS, w // 2), BF16),
        s2b=pltpu.VMEM((STEPS, RS_SPLIT, NZ, 2, ROWS, w // 2), BF16),
        r2a=pltpu.VMEM((STEPS, RS_SPLIT, NZ, ROWS, w // 2), BF16),
        r2b=pltpu.VMEM((STEPS, RS_SPLIT, NZ, ROWS, w // 2), BF16),
        s3=pltpu.VMEM((STEPS, RS_SPLIT, NZ, ROWS, w), BF16),
        r3=pltpu.VMEM((STEPS, RS_SPLIT, NZ - 1, ROWS, w), BF16),
        tot=pltpu.VMEM((STEPS, ROWS, width), F32),
        full=pltpu.VMEM((STEPS, NZ, 2, 2, 2, ROWS, width), BF16),
        rs_s=pltpu.SemaphoreType.DMA((STEPS * RS_SPLIT, 8)),
        rs_r=pltpu.SemaphoreType.DMA((STEPS * RS_SPLIT, 8)),
        ag_s=pltpu.SemaphoreType.DMA((STEPS * AG_SPLIT, 8)),
        ag_r=pltpu.SemaphoreType.DMA((STEPS * AG_SPLIT, 8)),
    )


EXCHANGE_NAMES = ("part", "rc", "s1", "r1a", "r1b", "s2a", "s2b", "r2a", "r2b", "s3", "r3", "tot", "full", "rs_s", "rs_r", "ag_s", "ag_r")


def run_exchange(place, b, width, produce, barrier_wait, finalize, consume):
    x, y, z, c = place.x, place.y, place.z, place.c
    sent = []

    def add(dst, left, right):
        dst[...] = (left[...].astype(F32) + right[...].astype(F32)).astype(BF16)

    def rs_stages(s, h):
        w = width // RS_SPLIT
        lo = h * w
        cols = pl.ds(lo, w)
        ca, cb = pl.ds(lo, w // 2), pl.ds(lo + w // 2, w // 2)
        n = s * RS_SPLIT + h
        ss, rs = b["rs_s"], b["rs_r"]
        live = {}

        def go(j, src, dst, dev):
            cp = remote(src, dst, ss.at[n, j], rs.at[n, j], dev)
            cp.start()
            live[j] = cp
            sent.append(cp)

        def st0():
            produce(s, h)
            barrier_wait()
            go(0, b["part"].at[s, :, :, :, 1 - c, :, cols], b["rc"].at[s, :, :, :, :, cols], place.sib)

        def st1():
            live[0].wait_recv()

            def body(i, _):
                add(b["s1"].at[s, i, :, :, :, cols], b["part"].at[s, i, :, :, c, :, cols], b["rc"].at[s, i, :, :, :, cols])
                return 0

            lax.fori_loop(0, NZ, body, 0)
            go(1, b["s1"].at[s, :, :, 1 - x, :, ca], b["r1a"].at[s, h], place.xpeer)
            go(2, b["s1"].at[s, :, 1 - y, :, :, cb], b["r1b"].at[s, h], place.ypeer)

        def st2():
            live[1].wait_recv()

            def body_a(i, _):
                add(b["s2a"].at[s, h, i], b["s1"].at[s, i, :, x, :, ca], b["r1a"].at[s, h, i])
                return 0

            lax.fori_loop(0, NZ, body_a, 0)
            go(3, b["s2a"].at[s, h, :, 1 - y], b["r2a"].at[s, h], place.ypeer)
            live[2].wait_recv()

            def body_b(i, _):
                add(b["s2b"].at[s, h, i], b["s1"].at[s, i, y, :, :, cb], b["r1b"].at[s, h, i])
                return 0

            lax.fori_loop(0, NZ, body_b, 0)
            go(4, b["s2b"].at[s, h, :, 1 - x], b["r2b"].at[s, h], place.xpeer)

        def st3():
            live[3].wait_recv()
            add(b["s3"].at[s, h, :, :, pl.ds(0, w // 2)], b["s2a"].at[s, h, :, y], b["r2a"].at[s, h])
            live[4].wait_recv()
            add(b["s3"].at[s, h, :, :, pl.ds(w // 2, w // 2)], b["s2b"].at[s, h, :, x], b["r2b"].at[s, h])
            for k in range(1, NZ):
                go(4 + k, b["s3"].at[s, h, lax.rem(z + k, NZ)], b["r3"].at[s, h, k - 1], place.zpeer(k))

        def st4():
            for k in range(1, NZ):
                live[4 + k].wait_recv()
            total = b["s3"][s, h, z].astype(F32)
            for k in range(1, NZ):
                total = total + b["r3"][s, h, k - 1].astype(F32)
            b["tot"][s, :, cols] = total

        return [st0, st1, st2, st3, st4]

    def ag_stages(s, h):
        w = width // AG_SPLIT
        lo = h * w
        cols = pl.ds(lo, w)
        ca, cb = pl.ds(lo, w // 2), pl.ds(lo + w // 2, w // 2)
        n = s * AG_SPLIT + h
        ss, rs = b["ag_s"], b["ag_r"]
        full = b["full"]
        live = {}

        def go(j, ref, dev):
            cp = remote(ref, ref, ss.at[n, j], rs.at[n, j], dev)
            cp.start()
            live[j] = cp
            sent.append(cp)

        def st0():
            if h == 0:
                finalize(s)
            for k in range(1, NZ):
                go(k - 1, full.at[s, z, y, x, c, :, cols], place.zpeer(k))

        def st1():
            for k in range(1, NZ):
                live[k - 1].wait_recv()
            go(3, full.at[s, :, y, x, c, :, ca], place.ypeer)
            go(4, full.at[s, :, y, x, c, :, cb], place.xpeer)

        def st2():
            live[3].wait_recv()
            go(5, full.at[s, :, :, x, c, :, ca], place.xpeer)
            live[4].wait_recv()
            go(6, full.at[s, :, y, :, c, :, cb], place.ypeer)

        def st3():
            live[5].wait_recv()
            live[6].wait_recv()
            go(7, full.at[s, :, :, :, c, :, cols], place.sib)

        def st4():
            live[7].wait_recv()
            if h == AG_SPLIT - 1:
                consume(s)

        return [st0, st1, st2, st3, st4]

    items = []
    for s in range(STEPS):
        for h in range(RS_SPLIT):
            k = s * RS_SPLIT + h
            for t, stage in enumerate(rs_stages(s, h)):
                items.append((k + t, k, stage))
        for h in range(AG_SPLIT):
            first = s * RS_SPLIT + RS_SPLIT - 1 + 4
            for t, stage in enumerate(ag_stages(s, h)):
                items.append((first + t, 0.5 + s * RS_SPLIT + RS_SPLIT - 1 + h * 0.1, stage))
    for _, _, stage in sorted(items, key=lambda e: (e[0], e[1])):
        stage()
    for cp in sent:
        cp.wait_send()


def front_kernel(vocab_dev, width, qkv_dev, ff_dev, tok_ref, gain_ref, embed_ref, w_ref, x_ref, qkv_ref, mlp_ref,
                 emb, hot, wq, wg, wu, sq, rq, local_sem, a_s, a_r, *bufs):
    b = dict(zip(EXCHANGE_NAMES, bufs))
    place = Place()
    me = place.me
    barrier = greet(place)
    half = width // RS_SPLIT
    loads = []
    for h in range(RS_SPLIT):
        cols = pl.ds(h * half, half)
        loads.append(pltpu.make_async_copy(embed_ref.at[:, cols], emb.at[:, cols], local_sem.at[h]))
    pieces = ((wq, 0, qkv_dev), (wg, qkv_dev, ff_dev), (wu, qkv_dev + ff_dev, ff_dev))
    for i, (dst, start, size) in enumerate(pieces):
        loads.append(pltpu.make_async_copy(w_ref.at[pl.ds(start, size), :], dst, local_sem.at[RS_SPLIT + i]))
    for cp in loads:
        cp.start()
    vocab_start = me * vocab_dev

    def produce(s, h):
        if s == 0:
            loads[h].wait()
        if h == 0:
            def build(i, _):
                rows = pl.ds(pl.multiple_of(i * 128, 128), 128)
                ids = tok_ref[rows, s:s + 1] - vocab_start
                lanes = lax.broadcasted_iota(jnp.int32, (128, vocab_dev), 1)
                hot[s, rows, :] = jnp.where(ids == lanes, 1.0, 0.0).astype(BF16)
                return 0

            lax.fori_loop(0, 4, build, 0)

        tile = 512
        per = half // tile

        def mul(i, _):
            zi, ni = lax.div(i, per), lax.rem(i, per)
            rows = pl.ds(pl.multiple_of(zi * 256, 256), 256)
            cols = pl.ds(pl.multiple_of(h * half + ni * tile, tile), tile)
            out = jnp.dot(hot[s, rows, :], emb[:, cols], preferred_element_type=F32).astype(BF16)
            b["part"][s, pl.ds(2 * zi, 2), :, :, :, :, cols] = out.reshape(2, 2, 2, 2, ROWS, tile)
            return 0

        lax.fori_loop(0, 2 * per, mul, 0)

    pending = [True]

    def barrier_wait():
        if pending[0]:
            pl.semaphore_wait(barrier, NDEV - 1)
            pending[0] = False

    def finalize(s):
        rows = b["tot"][s]
        x_ref[s] = rows.astype(BF16)
        b["full"][s, place.z, place.y, place.x, place.c] = norm_rows(rows, gain_ref[...].astype(F32))

    def send_qkv(s, k):
        to = place.peer(k)
        return remote(sq.at[s, to], rq.at[me, s], a_s.at[s, k], a_r.at[s, k], to)

    def consume(s):
        if s == 0:
            for cp in loads[RS_SPLIT:]:
                cp.wait()

        def mul(i, _):
            hid = b["full"][s, pl.ds(2 * i, 2)].reshape(256, width)
            qkv = dot_nt(hid, wq[...]).astype(BF16)
            sq[s, pl.ds(16 * i, 16)] = qkv.reshape(16, ROWS, qkv_dev)
            return 0

        lax.fori_loop(0, 2, mul, 0)
        rq[me, s] = sq[s, me]

        def send(k, _):
            send_qkv(s, k).start()
            return 0

        lax.fori_loop(1, NDEV, send, 0)

        def mlp(i, _):
            hid = b["full"][s, pl.ds(2 * i, 2)].reshape(256, width)
            gate = dot_nt(hid, wg[...]).astype(BF16).astype(F32)
            up = dot_nt(hid, wu[...]).astype(BF16).astype(F32)
            act = (gate * (1.0 / (1.0 + jnp.exp(-gate)))) * up
            mlp_ref[s, pl.ds(pl.multiple_of(256 * i, 256), 256), :] = act.astype(BF16)
            return 0

        lax.fori_loop(0, 2, mlp, 0)

    run_exchange(place, b, width, produce, barrier_wait, finalize, consume)
    for s in range(STEPS):
        def finish(k, _):
            cp = send_qkv(s, k)
            cp.wait_send()
            cp.wait_recv()
            return 0

        lax.fori_loop(1, NDEV, finish, 0)

    def copy_out(i, _):
        qkv_ref[i] = rq[i]
        return 0

    lax.fori_loop(0, NDEV, copy_out, 0)


def back_kernel(vocab_dev, width, attn_dev, ff_dev, scale, send_ref, mlp_ref, x_ref, gain_ref, next_ref, w_ref, embed_ref, out_ref,
                emb, wv, ac, r8, r4, local_sem, a_s, a_r, st_s, st_r, *bufs):
    b = dict(zip(EXCHANGE_NAMES, bufs))
    place = Place()
    me = place.me
    r8[...] = jnp.zeros_like(r8)
    r4[...] = jnp.zeros_like(r4)
    barrier = greet(place)
    load_w = pltpu.make_async_copy(w_ref, wv, local_sem.at[0])
    load_e = pltpu.make_async_copy(embed_ref, emb, local_sem.at[1])
    load_w.start()
    load_e.start()
    vocab_start = me * vocab_dev
    half = width // RS_SPLIT

    def send_attn(k):
        to = place.peer(k)
        return remote(send_ref.at[to], ac.at[:, me], a_s.at[k], a_r.at[k], to)

    ac[:, me] = send_ref[me]
    pl.semaphore_wait(barrier, NDEV - 1)

    def send(k, _):
        send_attn(k).start()
        return 0

    lax.fori_loop(1, NDEV, send, 0)
    load_w.wait()

    def arrive(k, _):
        send_attn(k).wait_recv()
        return 0

    lax.fori_loop(1, NDEV, arrive, 0)

    def produce(s, h):
        tile = 512
        per = half // tile

        def mul(i, _):
            zi, ni = lax.div(i, per), lax.rem(i, per)
            cols = pl.ds(pl.multiple_of(h * half + ni * tile, tile), tile)
            att = ac[s, pl.ds(16 * zi, 16)].reshape(256, attn_dev)
            mid = mlp_ref[s, pl.ds(pl.multiple_of(256 * zi, 256), 256), :]
            out = jnp.dot(att, wv[0:attn_dev, cols], preferred_element_type=F32)
            out = out + jnp.dot(mid, wv[attn_dev:attn_dev + ff_dev, cols], preferred_element_type=F32)
            b["part"][s, pl.ds(2 * zi, 2), :, :, :, :, cols] = out.astype(BF16).reshape(2, 2, 2, 2, ROWS, tile)
            return 0

        lax.fori_loop(0, 2 * per, mul, 0)

    def finalize(s):
        layer = b["tot"][s].astype(BF16).astype(F32)
        resid = x_ref[s].astype(F32) + layer
        b["full"][s, place.z, place.y, place.x, place.c] = norm_rows(resid, gain_ref[...].astype(F32))

    plane = lax.rem(me, 8)

    def send_plane(s, k):
        q = lax.rem(plane + k, 8)
        return remote(r8.at[s, plane], r8.at[s, plane], st_s.at[s, k], st_r.at[s, k], me - plane + q)

    def send_line(s, k):
        return remote(r4.at[s, place.z], r4.at[s, place.z], st_s.at[s, 8 + k], st_r.at[s, 8 + k], place.zpeer(k))

    def consume(s):
        if s == 0:
            load_e.wait()
        batch = NDEV * ROWS
        tile = 256
        nxt = next_ref[s] - vocab_start

        def mul(i, carry):
            top, den, hit = carry
            rows = pl.ds(pl.multiple_of(i * tile, tile), tile)
            zed = b["full"][s].reshape(batch, width)
            logits = dot_nt(emb[rows, :], zed) * scale
            new = jnp.maximum(top, jnp.max(logits, axis=0, keepdims=True))
            den = den * jnp.exp(top - new) + jnp.sum(jnp.exp(logits - new), axis=0, keepdims=True)
            ids = lax.broadcasted_iota(jnp.int32, (tile, batch), 0) + i * tile
            hit = hit + jnp.sum(jnp.where(ids == nxt, logits, 0.0), axis=0, keepdims=True)
            return new, den, hit

        zero = jnp.zeros((1, batch), F32)
        top, den, hit = lax.fori_loop(0, vocab_dev // tile, mul, (jnp.full((1, batch), -jnp.inf, F32), zero, zero))
        r8[s, plane, 0:1, :] = top
        r8[s, plane, 1:2, :] = den
        r8[s, plane, 2:3, :] = hit
        for k in range(1, 8):
            send_plane(s, k).start()

    def merge(buf, s, count):
        top = buf[s, 0, 0:1, :]
        for i in range(1, count):
            top = jnp.maximum(top, buf[s, i, 0:1, :])
        den = jnp.zeros_like(top)
        hit = jnp.zeros_like(top)
        for i in range(count):
            den = den + buf[s, i, 1:2, :] * jnp.exp(buf[s, i, 0:1, :] - top)
            hit = hit + buf[s, i, 2:3, :]
        return top, den, hit

    run_exchange(place, b, width, produce, lambda: None, finalize, consume)
    for s in range(STEPS):
        for k in range(1, 8):
            send_plane(s, k).wait_recv()
        top, den, hit = merge(r8, s, 8)
        r4[s, place.z, 0:1, :] = top
        r4[s, place.z, 1:2, :] = den
        r4[s, place.z, 2:3, :] = hit
        for k in range(1, NZ):
            send_line(s, k).start()
    for s in range(STEPS):
        for k in range(1, NZ):
            send_line(s, k).wait_recv()
        top, den, hit = merge(r4, s, NZ)
        out_ref[s] = hit - top - jnp.log(den)
    for s in range(STEPS):
        for k in range(1, 8):
            send_plane(s, k).wait_send()
        for k in range(1, NZ):
            send_line(s, k).wait_send()

    def finish(k, _):
        send_attn(k).wait_send()
        return 0

    lax.fori_loop(1, NDEV, finish, 0)


def attention_kernel(heads, lens_ref, q_ref, kn_ref, vn_ref, kc_ref, vc_ref, o_ref, ko_ref, vo_ref):
    first = lens_ref[pl.program_id(0)]
    ko_ref[...] = kc_ref[...]
    vo_ref[...] = vc_ref[...]
    for s in range(STEPS):
        pos = first + s
        base = pl.multiple_of(lax.div(pos, 16) * 16, 16)
        rows = lax.broadcasted_iota(jnp.int32, (16, ko_ref.shape[2]), 0) == pos - base
        ko_ref[0, pl.ds(base, 16), :] = jnp.where(rows, kn_ref[0, s:s + 1, :], ko_ref[0, pl.ds(base, 16), :])
        vo_ref[0, pl.ds(base, 16), :] = jnp.where(rows, vn_ref[0, s:s + 1, :], vo_ref[0, pl.ds(base, 16), :])
    scores = dot_nt(q_ref[0], ko_ref[0])
    times = lax.broadcasted_iota(jnp.int32, scores.shape, 1)
    limit = first + jnp.where(lax.broadcasted_iota(jnp.int32, scores.shape, 0) >= heads, 1, 0)
    scores = jnp.where(times <= limit, scores, -jnp.inf)
    scores = jnp.exp(scores - jnp.max(scores, axis=1, keepdims=True))
    probs = (scores / jnp.sum(scores, axis=1, keepdims=True)).astype(BF16)
    o_ref[0] = jnp.dot(probs, vo_ref[0], preferred_element_type=F32).astype(BF16)


def solution(mesh):
    def device_fn(tok_ids, next_ids, seq_lens, embed_loc, ln_gain, w_in_loc, w_out_loc, final_gain, k_loc, v_loc):
        steps, batch = tok_ids.shape
        vocab_dev, width = embed_loc.shape
        batch_dev, cache_len, head_dim = k_loc.shape
        in_dev, out_dev = w_in_loc.shape[1], w_out_loc.shape[0]
        kv_dev = 2 * head_dim // NDEV
        attn_dev = 2 * out_dev - in_dev + kv_dev
        ff_dev = out_dev - attn_dev
        qkv_dev = attn_dev + kv_dev
        attn_width = attn_dev * NDEV
        heads = attn_width // head_dim
        dev_index = lax.axis_index('tp')
        own_lens = lax.dynamic_slice_in_dim(seq_lens, dev_index * batch_dev, batch_dev)

        scratch = exchange_scratch(width)
        exchange = [scratch[name] for name in EXCHANGE_NAMES]
        vmem = pl.BlockSpec(memory_space=pltpu.VMEM)
        anym = pl.BlockSpec(memory_space=pl.ANY)
        dma = pltpu.SemaphoreType.DMA
        x_own, qkv_parts, mlp = pl.pallas_call(
            functools.partial(front_kernel, vocab_dev, width, qkv_dev, ff_dev),
            out_shape=(
                jax.ShapeDtypeStruct((steps, batch_dev, width), BF16),
                jax.ShapeDtypeStruct((NDEV, steps, batch_dev, qkv_dev), BF16),
                jax.ShapeDtypeStruct((steps, batch, ff_dev), BF16),
            ),
            in_specs=[vmem, vmem, anym, anym],
            out_specs=(vmem, vmem, vmem),
            scratch_shapes=[
                pltpu.VMEM((vocab_dev, width), BF16),
                pltpu.VMEM((steps, batch, vocab_dev), BF16),
                pltpu.VMEM((qkv_dev, width), BF16),
                pltpu.VMEM((ff_dev, width), BF16),
                pltpu.VMEM((ff_dev, width), BF16),
                pltpu.VMEM((steps, NDEV, batch_dev, qkv_dev), BF16),
                pltpu.VMEM((NDEV, steps, batch_dev, qkv_dev), BF16),
                dma((RS_SPLIT + 3,)),
                dma((steps, NDEV)),
                dma((steps, NDEV)),
            ] + exchange,
            compiler_params=pltpu.CompilerParams(collective_id=0, has_side_effects=True, vmem_limit_bytes=60 * 1024 * 1024),
            name="front",
        )(tok_ids.T, ln_gain.reshape(1, width), embed_loc, w_in_loc.T)

        qkv_own = qkv_parts.transpose(1, 2, 0, 3).reshape(steps, batch_dev, NDEV * qkv_dev)
        positions = own_lens[None, :] + jnp.arange(steps, dtype=own_lens.dtype)[:, None]
        queries = qkv_own[..., :attn_width].reshape(steps, batch_dev, heads, head_dim).astype(F32)
        q_rot = (rotary(queries, positions[..., None]) * head_dim ** -0.5).astype(BF16)
        q_rot = q_rot.transpose(1, 0, 2, 3).reshape(batch_dev, steps * heads, head_dim)
        k_new = rotary(qkv_own[..., attn_width:attn_width + head_dim].astype(F32), positions).astype(BF16).transpose(1, 0, 2)
        v_new = qkv_own[..., attn_width + head_dim:].transpose(1, 0, 2)

        def row(i, lens):
            return (i, 0, 0)

        cache_spec = pl.BlockSpec((1, cache_len, head_dim), row)
        attn, k_out, v_out = pl.pallas_call(
            functools.partial(attention_kernel, heads),
            out_shape=(
                jax.ShapeDtypeStruct((batch_dev, steps * heads, head_dim), BF16),
                jax.ShapeDtypeStruct(k_loc.shape, BF16),
                jax.ShapeDtypeStruct(v_loc.shape, BF16),
            ),
            grid_spec=pltpu.PrefetchScalarGridSpec(
                num_scalar_prefetch=1,
                grid=(batch_dev,),
                in_specs=[
                    pl.BlockSpec((1, steps * heads, head_dim), row),
                    pl.BlockSpec((1, steps, head_dim), row),
                    pl.BlockSpec((1, steps, head_dim), row),
                    cache_spec,
                    cache_spec,
                ],
                out_specs=(pl.BlockSpec((1, steps * heads, head_dim), row), cache_spec, cache_spec),
            ),
            compiler_params=pltpu.CompilerParams(vmem_limit_bytes=32 * 1024 * 1024),
            name="attention",
        )(own_lens, q_rot, k_new, v_new, k_loc, v_loc)

        attn_send = attn.reshape(batch_dev, steps, NDEV, attn_dev).transpose(2, 1, 0, 3)
        log_probs = pl.pallas_call(
            functools.partial(back_kernel, vocab_dev, width, attn_dev, ff_dev, width ** -0.5),
            out_shape=jax.ShapeDtypeStruct((steps, 1, batch), F32),
            in_specs=[vmem, vmem, vmem, vmem, vmem, anym, anym],
            out_specs=vmem,
            scratch_shapes=[
                pltpu.VMEM((vocab_dev, width), BF16),
                pltpu.VMEM((out_dev, width), BF16),
                pltpu.VMEM((steps, NDEV, batch_dev, attn_dev), BF16),
                pltpu.VMEM((steps, 8, 8, batch), F32),
                pltpu.VMEM((steps, NZ, 8, batch), F32),
                dma((2,)),
                dma((NDEV,)),
                dma((NDEV,)),
                dma((steps, 12)),
                dma((steps, 12)),
            ] + exchange,
            compiler_params=pltpu.CompilerParams(collective_id=1, has_side_effects=True, vmem_limit_bytes=60 * 1024 * 1024),
            name="back",
        )(attn_send, mlp, x_own, final_gain.reshape(1, width), next_ids.reshape(steps, 1, batch), w_out_loc, embed_loc)
        return log_probs.reshape(steps, batch), k_out, v_out

    cache_spec = P('tp', None, None)
    return jax.shard_map(device_fn, mesh=mesh, in_specs=(P(), P(), P(), P('tp', None), P(), P(None, 'tp'), P('tp', None), P(), cache_spec, cache_spec), out_specs=(P(), cache_spec, cache_spec), check_vma=False)
```

time: 545 us -> 193 us (0.35)
  waiting for transfers between devices: 297 us -> 0 us
  Pallas kernels: 0 us -> 176 us
  blocking collectives: 77.9 us -> 0 us
  matrix products: 55.1 us -> 0 us
  other arithmetic: 39.5 us -> 0.96 us
  local copies, waits for them, and re-layouts: 42 us -> 15.6 us
  starting transfers between devices: 17.1 us -> 0 us
  between operations: 14.5 us -> 0.73 us
    psum x2 -> x0, waiting for transfers between devices: 282 us -> none  [the longest x1 143 us: device_fn(): lax.psum(jnp.where(tok_here[:, None], emb_rows, jnp.zeros_like(emb_rows))...]
    pallas_call x0 -> x3, Pallas kernels: none -> 176 us  [the longest x1 87.9 us: device_fn(): pl.pallas_call(functools.partial(back_kernel, vocab_dev, width, attn_dev,...]
    dot_general x8 -> x0, matrix products: 39.6 us -> none  [the longest x2 15.9 us: device_fn(): jnp.einsum('bd,vd->bv', final_normed, embed_loc, preferred_element_type=j...]
    psum x1 -> x0, blocking collectives: 39.3 us -> none  [device_fn(): lax.psum(jnp.sum(jnp.exp(logits - row_max[:, None]), axis=1), 'tp')]
    pmax x1 -> x0, blocking collectives: 38.6 us -> none  [device_fn(): row_max = lax.pmax(jnp.max(logits, axis=1), 'tp')]
    gather x4 -> x0, local copies, waits for them, and re-layouts: 34.9 us -> none  [the longest x2 17.6 us: device_fn(): jnp.take(embed_loc, jnp.clip(local_ids, 0, vocab_dev - 1), axis=0)]
    select_n x10 -> x0, other arithmetic: 19 us -> none  [the longest x1 13.9 us: device_fn(): k_loc = jnp.where(write_mask, k_new[:, None, :], k_loc)]
    all_to_all x4 -> x0, starting transfers between devices: 16.8 us -> none  [the longest x2 8.4 us: device_fn(): qkv_own = lax.all_to_all(proj_out[:, :qkv_dev], 'tp', 0, 1, tiled=True)]
  transfers between devices with their start and end apart: 6 -> 0, of which waited for: 5 -> 0; matrix products, arithmetic and copies ran while one was open for 6% -> 0% of each run, Pallas kernels for 0% -> 0%
where the time goes in v1:
time: 193 us
  Pallas kernels  176 us (91%)
  local copies, waits for them, and re-layouts  15.6 us (8%)
    pallas_call x1, Pallas kernels, device_fn(): pl.pallas_call(functools.partial(back_kernel, vocab_dev, width, attn_dev,...  87.9 us
    pallas_call x1, Pallas kernels, device_fn(): pl.pallas_call(functools.partial(front_kernel, vocab_dev, width, qkv_dev,...  75 us
    pallas_call x1, Pallas kernels, device_fn(): pl.pallas_call(functools.partial(attention_kernel, heads), out_shape=(jax...  12.7 us
    unnamed x10, local copies, waits for them, and re-layouts  9.57 us

profile of v1, /device:TPU:0, one launch (start us, length us, event | category | flops | bytes accessed | tf_op | source)
XLA Modules:
  0.0 192.9 jit_solution(14544507869704465058)
XLA Ops:
  0.6 0.8 dynamic_slice.3.lens_ref
  1.4 0.1 add_convert_fusion.1
  1.5 1.5 copy.18
  3.0 1.3 reshape.93.gain_ref
  4.3 75.0 %front.1 = (bf16[2,16,2048]{2,1,0:T(8,128)(2,1)}, bf16[32,2,16,72]{3,2,1,0:T(8,128)(2,1)}, bf16[2,512,256]{2,1,0:T(8,128)(2,1)}) custom-call(s32[512,2]{1,0:T(8,128)} %bitcast.25, bf16[1,2048]{1,0:T(2,128)(2,1)} %reshape.93.gain_ref, bf16[1536,2048]{1,0:T(8,128)(2,1)} %embed_ref.3, bf16[584,2048]{1,0:T(8,128)(2,1)} %bitcast.23), custom_call_target="tpu_custom_call" | custom-call | tf_op jit(solution)/shard_map/front/pallas_call | solution.py:515
  79.3 1.1 copy.19
  80.4 0.5 reshape.94
  80.9 0.3 subtract_convert_fusion
  81.2 0.1 slice_convert_fusion
  81.4 0.2 reshape.100
  81.6 0.2 multiply_subtract_fusion
  81.8 0.1 fusion
  81.9 0.1 maximum_bitcast_fusion.kn_ref
  82.0 0.0 copy-start
  82.0 3.4 %copy-done = bf16[16,2048,128]{2,1,0:T(8,128)(2,1)S(1)} copy-done((bf16[16,2048,128]{2,1,0:T(8,128)(2,1)S(1)}, bf16[16,2048,128]{2,1,0:T(8,128)(2,1)}, u32[]{:S(2)}) %copy-start) | copy-done | bytes 8388632
  85.4 0.0 copy-start.1
  85.4 3.4 %copy-done.1 = bf16[16,2048,128]{2,1,0:T(8,128)(2,1)S(1)} copy-done((bf16[16,2048,128]{2,1,0:T(8,128)(2,1)S(1)}, bf16[16,2048,128]{2,1,0:T(8,128)(2,1)}, u32[]{:S(2)}) %copy-start.1) | copy-done | bytes 8388632
  88.8 0.0 copy-start.2
  88.8 0.0 copy-start.3
  88.8 12.7 %attention.1 = (bf16[16,32,128]{2,1,0:T(8,128)(2,1)S(1)}, bf16[16,2048,128]{2,1,0:T(8,128)(2,1)}, bf16[16,2048,128]{2,1,0:T(8,128)(2,1)}) custom-call(s32[16]{0:T(128)S(1)} %dynamic_slice.3.lens_ref, bf16[16,32,128]{2,1,0:T(8,128)(2,1)S(1)} %bitcast.22, bf16[16,2,128]{2,1,0:T(2,128)(2,1)S(1)} %maximum_bitcast_fusion.kn_ref, ...), custom_call_target="tpu_custom_call" | custom-call | tf_op jit(solution)/shard_map/attention/pallas_call | solution.py:552
  101.5 0.1 reshape.96
  101.6 0.9 copy.25
  102.5 0.0 copy-done.2
  102.5 0.6 reshape.97.gain_ref
  103.1 0.0 copy-done.3
  103.1 0.6 reshape.98.next_ref
  103.7 87.9 %back.1 = f32[2,1,512]{2,1,0:T(1,128)} custom-call(bf16[32,2,16,64]{3,2,1,0:T(8,128)(2,1)} %bitcast.24, bf16[2,512,256]{2,1,0:T(8,128)(2,1)} %get-tuple-element.11.mlp_ref, bf16[2,16,2048]{2,1,0:T(8,128)(2,1)} %get-tuple-element.12.x_ref, bf16[1,2048]{1,0:T(2,128)(2,1)} %reshape.97.gain_ref, s32[2,1,512]{2,1,0:T(1,128)} %reshape.98.next_ref, ...), custom_call_target="tpu_custom_call" | custom-call | tf_op jit(solution)/shard_map/back/pallas_call | solution.py:576
  191.7 1.3 copy.26
  (2 shorter events, 0.0 us)
Async XLA Ops:
  82.0 3.4 %copy-start = (bf16[16,2048,128]{2,1,0:T(8,128)(2,1)S(1)}, bf16[16,2048,128]{2,1,0:T(8,128)(2,1)}, u32[]{:S(2)}) copy-start(bf16[16,2048,128]{2,1,0:T(8,128)(2,1)} %kc_ref.1) | copy-start | bytes 25165828
  85.4 3.4 %copy-start.1 = (bf16[16,2048,128]{2,1,0:T(8,128)(2,1)S(1)}, bf16[16,2048,128]{2,1,0:T(8,128)(2,1)}, u32[]{:S(2)}) copy-start(bf16[16,2048,128]{2,1,0:T(8,128)(2,1)} %vc_ref.1) | copy-start | bytes 25165828
  88.8 13.7 %copy-start.2 = (bf16[2048]{0:T(1024)(128)(2,1)S(1)}, bf16[2048]{0:T(1024)(128)(2,1)}, u32[]{:S(2)}) copy-start(bf16[2048]{0:T(1024)(128)(2,1)} %param.17) | copy-start | bytes 12292
  88.8 14.3 %copy-start.3 = (s32[2,512]{1,0:T(2,128)S(1)}, s32[2,512]{1,0:T(2,128)}, u32[]{:S(2)}) copy-start(s32[2,512]{1,0:T(2,128)} %param.11) | copy-start | bytes 12292

commit v2 on v1

v2 whole, which is shorter than its diff:
```python
import functools

import jax
import jax.numpy as jnp
from jax import lax
from jax.experimental import pallas as pl
from jax.experimental.pallas import tpu as pltpu
from jax.sharding import PartitionSpec as P

ROPE_BASE = 10000.0
NORM_EPS = 1e-6
MESH_ID = pl.DeviceIdType.MESH
ROWS = 8
NZ = 4
NDEV = 32
STEPS = 2
HALVES = 2
PIECES = STEPS * HALVES
FRONT_ORDER = (
    "r00 r10 r01 r11 r20 r30 r02 r12 r21 r03 r13 r31 r04 r22 g00 r14 g10 r32 r23 g01 "
    "r33 g11 r24 g20 g12 g02 r34 g30 g21 g03 g31 g13 g22 g32 g04 g14 g23 g24 g33 g34"
)
BACK_ORDER = (
    "r00 r01 r10 r11 r20 r30 r02 r12 r21 r31 r03 r13 r04 g00 r32 r14 g10 r22 r33 g01 "
    "g11 r23 g02 r34 g30 r24 g20 g12 g03 g31 g21 g13 g32 g04 g22 g33 g14 g23 g34 g24"
)
KERNEL_VMEM = 60 * 1024 * 1024
BF16 = jnp.bfloat16
F32 = jnp.float32


def rotary(vectors, positions):
    half_dim = vectors.shape[-1] // 2
    inv_freq = ROPE_BASE ** (-jnp.arange(half_dim, dtype=jnp.float32) / half_dim)
    angles = positions.astype(jnp.float32)[..., None] * inv_freq
    cosine = jnp.cos(angles)
    sine_val = jnp.sin(angles)
    first_half = vectors[..., :half_dim]
    second_half = vectors[..., half_dim:]
    return jnp.concatenate([first_half * cosine - second_half * sine_val, second_half * cosine + first_half * sine_val], axis=-1)


def norm_rows(values, gain):
    centered = values - jnp.mean(values, axis=-1, keepdims=True)
    variance = jnp.mean(jnp.square(centered), axis=-1, keepdims=True)
    return (centered * lax.rsqrt(variance + NORM_EPS) * gain).astype(BF16)


def dot_nt(a, b):
    return lax.dot_general(a, b, (((1,), (1,)), ((), ())), preferred_element_type=F32)


class Place:
    def __init__(self):
        self.me = lax.axis_index("tp")
        self.c = lax.rem(self.me, 2)
        self.x = lax.rem(lax.div(self.me, 2), 2)
        self.y = lax.rem(lax.div(self.me, 4), 2)
        self.z = lax.div(self.me, 8)
        self.sib = self.me + 1 - 2 * self.c
        self.xpeer = self.me + 2 * (1 - 2 * self.x)
        self.ypeer = self.me + 4 * (1 - 2 * self.y)

    def zpeer(self, k):
        return lax.rem(self.me + 8 * k, NDEV)

    def peer(self, k):
        return lax.rem(self.me + k, NDEV)


def remote(src, dst, ssem, rsem, dev):
    return pltpu.make_async_remote_copy(src_ref=src, dst_ref=dst, send_sem=ssem, recv_sem=rsem, device_id=(dev,), device_id_type=MESH_ID)


def greet(place):
    barrier = pltpu.get_barrier_semaphore()

    def body(k, _):
        pl.semaphore_signal(barrier, inc=1, device_id=(place.peer(k),), device_id_type=MESH_ID)
        return 0

    lax.fori_loop(1, NDEV, body, 0)
    return barrier


def exchange_scratch(width):
    half = width // 2
    return dict(
        part=pltpu.VMEM((PIECES, NZ, 2, 2, 2, ROWS, width), BF16),
        rc=pltpu.VMEM((PIECES, NZ, 2, 2, ROWS, width), BF16),
        s1=pltpu.VMEM((PIECES, NZ, 2, 2, ROWS, width), BF16),
        r1a=pltpu.VMEM((PIECES, NZ, 2, ROWS, half), BF16),
        r1b=pltpu.VMEM((PIECES, NZ, 2, ROWS, half), BF16),
        s2a=pltpu.VMEM((PIECES, NZ, 2, ROWS, half), BF16),
        s2b=pltpu.VMEM((PIECES, NZ, 2, ROWS, half), BF16),
        r2a=pltpu.VMEM((PIECES, NZ, ROWS, half), BF16),
        r2b=pltpu.VMEM((PIECES, NZ, ROWS, half), BF16),
        s3=pltpu.VMEM((PIECES, NZ, ROWS, width), BF16),
        r3=pltpu.VMEM((PIECES, NZ - 1, ROWS, width), BF16),
        full=pltpu.VMEM((PIECES, NZ, 2, 2, 2, ROWS, width), BF16),
        rows=pltpu.VMEM((NDEV * ROWS, width), BF16),
        rs_s=pltpu.SemaphoreType.DMA((PIECES, 8)),
        rs_r=pltpu.SemaphoreType.DMA((PIECES, 8)),
        ag_s=pltpu.SemaphoreType.DMA((PIECES, 8)),
        ag_r=pltpu.SemaphoreType.DMA((PIECES, 8)),
    )


EXCHANGE_NAMES = ("part", "rc", "s1", "r1a", "r1b", "s2a", "s2b", "r2a", "r2b", "s3", "r3", "full", "rows", "rs_s", "rs_r", "ag_s", "ag_r")


def run_exchange(place, b, width, order, produce, barrier_wait, finalize, consume):
    x, y, z, c = place.x, place.y, place.z, place.c
    half = width // 2
    ca, cb = pl.ds(0, half), pl.ds(half, half)
    full = b["full"]
    sent = []

    def add(dst, left, right):
        dst[...] = (left[...].astype(F32) + right[...].astype(F32)).astype(BF16)

    def add_z(dst, left, right):
        def body(i, _):
            add(dst(i), left(i), right(i))
            return 0

        lax.fori_loop(0, NZ, body, 0)

    def rs_stages(n):
        live = {}

        def go(j, src, dst, dev):
            cp = remote(src, dst, b["rs_s"].at[n, j], b["rs_r"].at[n, j], dev)
            cp.start()
            live[j] = cp
            sent.append(cp)

        def st0():
            produce(n)
            barrier_wait()
            go(0, b["part"].at[n, :, :, :, 1 - c], b["rc"].at[n], place.sib)

        def st1():
            live[0].wait_recv()
            add_z(lambda i: b["s1"].at[n, i], lambda i: b["part"].at[n, i, :, :, c], lambda i: b["rc"].at[n, i])
            go(1, b["s1"].at[n, :, :, 1 - x, :, ca], b["r1a"].at[n], place.xpeer)
            go(2, b["s1"].at[n, :, 1 - y, :, :, cb], b["r1b"].at[n], place.ypeer)

        def st2():
            live[1].wait_recv()
            add_z(lambda i: b["s2a"].at[n, i], lambda i: b["s1"].at[n, i, :, x, :, ca], lambda i: b["r1a"].at[n, i])
            go(3, b["s2a"].at[n, :, 1 - y], b["r2a"].at[n], place.ypeer)
            live[2].wait_recv()
            add_z(lambda i: b["s2b"].at[n, i], lambda i: b["s1"].at[n, i, y, :, :, cb], lambda i: b["r1b"].at[n, i])
            go(4, b["s2b"].at[n, :, 1 - x], b["r2b"].at[n], place.xpeer)

        def st3():
            live[3].wait_recv()
            add(b["s3"].at[n, :, :, ca], b["s2a"].at[n, :, y], b["r2a"].at[n])
            live[4].wait_recv()
            add(b["s3"].at[n, :, :, cb], b["s2b"].at[n, :, x], b["r2b"].at[n])
            for k in range(1, NZ):
                go(4 + k, b["s3"].at[n, lax.rem(z + k, NZ)], b["r3"].at[n, k - 1], place.zpeer(k))

        def st4():
            for k in range(1, NZ):
                live[4 + k].wait_recv()

        return [st0, st1, st2, st3, st4]

    def ag_stages(n):
        live = {}

        def go(j, ref, dev):
            cp = remote(ref, ref, b["ag_s"].at[n, j], b["ag_r"].at[n, j], dev)
            cp.start()
            live[j] = cp
            sent.append(cp)

        def st0():
            total = b["s3"][n, z].astype(F32)
            for k in range(1, NZ):
                total = total + b["r3"][n, k - 1].astype(F32)
            full[n, z, y, x, c] = finalize(n, total)
            for k in range(1, NZ):
                go(k - 1, full.at[n, z, y, x, c], place.zpeer(k))

        def st1():
            for k in range(1, NZ):
                live[k - 1].wait_recv()
            go(3, full.at[n, :, y, x, c, :, ca], place.ypeer)
            go(4, full.at[n, :, y, x, c, :, cb], place.xpeer)

        def st2():
            live[3].wait_recv()
            go(5, full.at[n, :, :, x, c, :, ca], place.xpeer)
            live[4].wait_recv()
            go(6, full.at[n, :, y, :, c, :, cb], place.ypeer)

        def st3():
            live[5].wait_recv()
            live[6].wait_recv()
            go(7, full.at[n, :, :, :, c], place.sib)

        def st4():
            live[7].wait_recv()

            def body(i, _):
                block = full[n, i].astype(F32).reshape(8 * ROWS, width).astype(BF16)
                b["rows"][pl.ds(pl.multiple_of(i * 8 * ROWS, 8 * ROWS), 8 * ROWS), :] = block
                return 0

            lax.fori_loop(0, NZ, body, 0)
            consume(n)

        return [st0, st1, st2, st3, st4]

    stages = {"r": [rs_stages(n) for n in range(PIECES)], "g": [ag_stages(n) for n in range(PIECES)]}
    for item in order.split():
        with jax.named_scope(item):
            stages[item[0]][int(item[1])][int(item[2])]()
    for cp in sent:
        cp.wait_send()


def front_kernel(vocab_dev, width, qkv_dev, ff_dev, tok_ref, gain_ref, embed_ref, w_ref, x_ref, qkv_ref, mlp_ref,
                 emb, ids, hot, wq, wg, wu, sq, rq, local_sem, a_s, a_r, *bufs):
    b = dict(zip(EXCHANGE_NAMES, bufs))
    place = Place()
    me = place.me
    barrier = greet(place)
    batch = NDEV * HALVES * ROWS
    total = NDEV * ROWS
    tile = 512
    loads = []
    for h in range(width // tile):
        cols = pl.ds(h * tile, tile)
        loads.append(pltpu.make_async_copy(embed_ref.at[:, cols], emb.at[:, cols], local_sem.at[h]))
    pieces = ((wq, 0, qkv_dev), (wg, qkv_dev, ff_dev), (wu, qkv_dev + ff_dev, ff_dev))
    for i, (dst, start, size) in enumerate(pieces):
        loads.append(pltpu.make_async_copy(w_ref.at[pl.ds(start, size), :], dst, local_sem.at[width // tile + i]))
    for cp in loads:
        cp.start()
    vocab_start = me * vocab_dev
    for s in range(STEPS):
        row = jnp.broadcast_to((tok_ref[s:s + 1, :] - vocab_start).astype(F32), (8, batch))
        ids[s] = row.T.astype(jnp.int32).reshape(NDEV, HALVES, ROWS, 8)

    def produce(n):
        col = ids[n // HALVES, :, n % HALVES].reshape(total, 8)
        for i in range(2):
            lanes = lax.broadcasted_iota(jnp.int32, (total // 2, vocab_dev), 1)
            mine = col[i * total // 2:(i + 1) * total // 2, 0:1]
            hot[pl.ds(i * total // 2, total // 2), :] = jnp.where(mine == lanes, 1.0, 0.0).astype(BF16)
        for h in range(width // tile):
            cols = pl.ds(h * tile, tile)
            if n == 0:
                loads[h].wait()
            out = jnp.dot(hot[...], emb[:, cols], preferred_element_type=F32)
            b["part"][n, :, :, :, :, :, cols] = out.reshape(NZ, 2, 2, 2, ROWS, tile).astype(BF16)

    pending = [True]

    def barrier_wait():
        if pending[0]:
            pl.semaphore_wait(barrier, NDEV - 1)
            pending[0] = False

    def finalize(n, rows):
        x_ref[n] = rows.astype(BF16)
        return norm_rows(rows, gain_ref[...].astype(F32))

    def send_qkv(s, k):
        to = place.peer(k)
        pair = pl.ds(HALVES * s, HALVES)
        return remote(sq.at[pair, to], rq.at[me, pair], a_s.at[s, k], a_r.at[s, k], to)

    def consume(n):
        if n == 0:
            for cp in loads[width // tile:]:
                cp.wait()
        qkv = dot_nt(b["rows"][...], wq[...])
        sq[n] = qkv.reshape(NDEV, ROWS, qkv_dev).astype(BF16)
        rq[me, n] = sq[n, me]
        if n % HALVES == HALVES - 1:
            def send(k, _):
                send_qkv(n // HALVES, k).start()
                return 0

            lax.fori_loop(1, NDEV, send, 0)
        gate = dot_nt(b["rows"][...], wg[...]).astype(BF16).astype(F32)
        up = dot_nt(b["rows"][...], wu[...]).astype(BF16).astype(F32)
        mlp_ref[n] = ((gate * (1.0 / (1.0 + jnp.exp(-gate)))) * up).astype(BF16)

    run_exchange(place, b, width, FRONT_ORDER, produce, barrier_wait, finalize, consume)
    with jax.named_scope("qkv_arrive"):
        for s in range(STEPS):
            def finish(k, _):
                cp = send_qkv(s, k)
                cp.wait_send()
                cp.wait_recv()
                return 0

            lax.fori_loop(1, NDEV, finish, 0)

    with jax.named_scope("qkv_out"):
        def copy_out(i, _):
            qkv_ref[i] = rq[i]
            return 0

        lax.fori_loop(0, NDEV, copy_out, 0)


def back_kernel(vocab_dev, width, attn_dev, ff_dev, scale, send_ref, mlp_ref, x_ref, gain_ref, next_ref, w_ref, embed_ref, out_ref,
                emb, wv, ac, r8, r4, local_sem, a_s, a_r, st_s, st_r, *bufs):
    b = dict(zip(EXCHANGE_NAMES, bufs))
    place = Place()
    me = place.me
    r8[...] = jnp.zeros_like(r8)
    r4[...] = jnp.zeros_like(r4)
    barrier = greet(place)
    load_w = pltpu.make_async_copy(w_ref, wv, local_sem.at[0])
    load_e = pltpu.make_async_copy(embed_ref, emb, local_sem.at[1])
    load_w.start()
    load_e.start()
    vocab_start = me * vocab_dev
    total = NDEV * ROWS

    def send_attn(k):
        to = place.peer(k)
        return remote(send_ref.at[to], ac.at[:, me], a_s.at[k], a_r.at[k], to)

    ac[:, me] = send_ref[me]
    with jax.named_scope("barrier"):
        pl.semaphore_wait(barrier, NDEV - 1)

    def send(k, _):
        send_attn(k).start()
        return 0

    with jax.named_scope("attn_send"):
        lax.fori_loop(1, NDEV, send, 0)
        load_w.wait()

    def arrive(k, _):
        send_attn(k).wait_recv()
        return 0

    with jax.named_scope("attn_arrive"):
        lax.fori_loop(1, NDEV, arrive, 0)

    def produce(n):
        tile = 512
        att = ac[n].astype(F32).reshape(total, attn_dev).astype(BF16)

        def mul(i, _):
            cols = pl.ds(pl.multiple_of(i * tile, tile), tile)
            out = jnp.dot(att, wv[0:attn_dev, cols], preferred_element_type=F32)
            out = out + jnp.dot(mlp_ref[n], wv[attn_dev:attn_dev + ff_dev, cols], preferred_element_type=F32)
            b["part"][n, :, :, :, :, :, cols] = out.reshape(NZ, 2, 2, 2, ROWS, tile).astype(BF16)
            return 0

        lax.fori_loop(0, width // tile, mul, 0)

    def finalize(n, rows):
        resid = x_ref[n].astype(F32) + rows.astype(BF16).astype(F32)
        return norm_rows(resid, gain_ref[...].astype(F32))

    plane = lax.rem(me, 8)

    def send_plane(n, k):
        q = lax.rem(plane + k, 8)
        return remote(r8.at[n, plane], r8.at[n, plane], st_s.at[n, k], st_r.at[n, k], me - plane + q)

    def send_line(n, k):
        return remote(r4.at[n, place.z], r4.at[n, place.z], st_s.at[n, 8 + k], st_r.at[n, 8 + k], place.zpeer(k))

    def consume(n):
        if n == 0:
            load_e.wait()
        tile = 512
        nxt = next_ref[n:n + 1, :] - vocab_start

        def mul(i, carry):
            top, den, hit = carry
            rows = pl.ds(pl.multiple_of(i * tile, tile), tile)
            logits = dot_nt(emb[rows, :], b["rows"][...]) * scale
            new = jnp.maximum(top, jnp.max(logits, axis=0, keepdims=True))
            den = den * jnp.exp(top - new) + jnp.sum(jnp.exp(logits - new), axis=0, keepdims=True)
            ids = lax.broadcasted_iota(jnp.int32, (tile, total), 0) + i * tile
            hit = hit + jnp.sum(jnp.where(ids == nxt, logits, 0.0), axis=0, keepdims=True)
            return new, den, hit

        zero = jnp.zeros((1, total), F32)
        top, den, hit = lax.fori_loop(0, vocab_dev // tile, mul, (jnp.full((1, total), -jnp.inf, F32), zero, zero))
        r8[n, plane, 0:1, :] = top
        r8[n, plane, 1:2, :] = den
        r8[n, plane, 2:3, :] = hit
        for k in range(1, 8):
            send_plane(n, k).start()

    def merge(buf, n, count):
        top = buf[n, 0, 0:1, :]
        for i in range(1, count):
            top = jnp.maximum(top, buf[n, i, 0:1, :])
        den = jnp.zeros_like(top)
        hit = jnp.zeros_like(top)
        for i in range(count):
            den = den + buf[n, i, 1:2, :] * jnp.exp(buf[n, i, 0:1, :] - top)
            hit = hit + buf[n, i, 2:3, :]
        return top, den, hit

    run_exchange(place, b, width, BACK_ORDER, produce, lambda: None, finalize, consume)
    last = [int(item[1]) for item in BACK_ORDER.split() if item[0] == "g" and item[2] == "4"]
    for n in last:
        with jax.named_scope("plane"):
            for k in range(1, 8):
                send_plane(n, k).wait_recv()
            top, den, hit = merge(r8, n, 8)
            r4[n, place.z, 0:1, :] = top
            r4[n, place.z, 1:2, :] = den
            r4[n, place.z, 2:3, :] = hit
            for k in range(1, NZ):
                send_line(n, k).start()
    for n in last:
        with jax.named_scope("line"):
            for k in range(1, NZ):
                send_line(n, k).wait_recv()
            top, den, hit = merge(r4, n, NZ)
            out_ref[n:n + 1, :] = hit - top - jnp.log(den)
    for n in range(PIECES):
        for k in range(1, 8):
            send_plane(n, k).wait_send()
        for k in range(1, NZ):
            send_line(n, k).wait_send()

    def finish(k, _):
        send_attn(k).wait_send()
        return 0

    lax.fori_loop(1, NDEV, finish, 0)


def attention_kernel(heads, lens_ref, q_ref, kn_ref, vn_ref, kc_ref, vc_ref, o_ref, ko_ref, vo_ref):
    first = lens_ref[pl.program_id(0)]
    ko_ref[...] = kc_ref[...]
    vo_ref[...] = vc_ref[...]
    for s in range(STEPS):
        pos = first + s
        base = pl.multiple_of(lax.div(pos, 16) * 16, 16)
        rows = lax.broadcasted_iota(jnp.int32, (16, ko_ref.shape[2]), 0) == pos - base
        ko_ref[0, pl.ds(base, 16), :] = jnp.where(rows, kn_ref[0, s:s + 1, :], ko_ref[0, pl.ds(base, 16), :])
        vo_ref[0, pl.ds(base, 16), :] = jnp.where(rows, vn_ref[0, s:s + 1, :], vo_ref[0, pl.ds(base, 16), :])
    scores = dot_nt(q_ref[0], ko_ref[0])
    times = lax.broadcasted_iota(jnp.int32, scores.shape, 1)
    limit = first + jnp.where(lax.broadcasted_iota(jnp.int32, scores.shape, 0) >= heads, 1, 0)
    scores = jnp.where(times <= limit, scores, -jnp.inf)
    scores = jnp.exp(scores - jnp.max(scores, axis=1, keepdims=True))
    probs = (scores / jnp.sum(scores, axis=1, keepdims=True)).astype(BF16)
    o_ref[0] = jnp.dot(probs, vo_ref[0], preferred_element_type=F32).astype(BF16)


def solution(mesh):
    def device_fn(tok_ids, next_ids, seq_lens, embed_loc, ln_gain, w_in_loc, w_out_loc, final_gain, k_loc, v_loc):
        steps, batch = tok_ids.shape
        vocab_dev, width = embed_loc.shape
        batch_dev, cache_len, head_dim = k_loc.shape
        in_dev, out_dev = w_in_loc.shape[1], w_out_loc.shape[0]
        kv_dev = 2 * head_dim // NDEV
        attn_dev = 2 * out_dev - in_dev + kv_dev
        ff_dev = out_dev - attn_dev
        qkv_dev = attn_dev + kv_dev
        attn_width = attn_dev * NDEV
        heads = attn_width // head_dim
        dev_index = lax.axis_index('tp')
        own_lens = lax.dynamic_slice_in_dim(seq_lens, dev_index * batch_dev, batch_dev)

        scratch = exchange_scratch(width)
        exchange = [scratch[name] for name in EXCHANGE_NAMES]
        vmem = pl.BlockSpec(memory_space=pltpu.VMEM)
        anym = pl.BlockSpec(memory_space=pltpu.HBM)
        dma = pltpu.SemaphoreType.DMA
        pair_dims = (steps, NDEV, HALVES, ROWS)
        piece_rows = NDEV * ROWS
        x_own, qkv_parts, mlp = pl.pallas_call(
            functools.partial(front_kernel, vocab_dev, width, qkv_dev, ff_dev),
            out_shape=(
                jax.ShapeDtypeStruct((PIECES, ROWS, width), BF16),
                jax.ShapeDtypeStruct((NDEV, PIECES, ROWS, qkv_dev), BF16),
                jax.ShapeDtypeStruct((PIECES, piece_rows, ff_dev), BF16),
            ),
            in_specs=[vmem, vmem, anym, anym],
            out_specs=(vmem, vmem, vmem),
            scratch_shapes=[
                pltpu.VMEM((vocab_dev, width), BF16),
                pltpu.VMEM((steps, NDEV, HALVES, ROWS, 8), jnp.int32),
                pltpu.VMEM((piece_rows, vocab_dev), BF16),
                pltpu.VMEM((qkv_dev, width), BF16),
                pltpu.VMEM((ff_dev, width), BF16),
                pltpu.VMEM((ff_dev, width), BF16),
                pltpu.VMEM((PIECES, NDEV, ROWS, qkv_dev), BF16),
                pltpu.VMEM((NDEV, PIECES, ROWS, qkv_dev), BF16),
                dma((8,)),
                dma((steps, NDEV)),
                dma((steps, NDEV)),
            ] + exchange,
            compiler_params=pltpu.CompilerParams(collective_id=0, has_side_effects=True, vmem_limit_bytes=KERNEL_VMEM),
            cost_estimate=pl.CostEstimate(flops=40_000_000_000, bytes_accessed=8_000_000, transcendentals=0),
            name="front",
        )(tok_ids, ln_gain.reshape(1, width), embed_loc, w_in_loc.T)

        qkv_own = qkv_parts.reshape(NDEV, steps, batch_dev, qkv_dev).transpose(1, 2, 0, 3).reshape(steps, batch_dev, NDEV * qkv_dev)
        positions = own_lens[None, :] + jnp.arange(steps, dtype=own_lens.dtype)[:, None]
        queries = qkv_own[..., :attn_width].reshape(steps, batch_dev, heads, head_dim).astype(F32)
        q_rot = (rotary(queries, positions[..., None]) * head_dim ** -0.5).astype(BF16)
        q_rot = q_rot.transpose(1, 0, 2, 3).reshape(batch_dev, steps * heads, head_dim)
        k_new = rotary(qkv_own[..., attn_width:attn_width + head_dim].astype(F32), positions).astype(BF16).transpose(1, 0, 2)
        v_new = qkv_own[..., attn_width + head_dim:].transpose(1, 0, 2)

        def row(i, lens):
            return (i, 0, 0)

        cache_spec = pl.BlockSpec((1, cache_len, head_dim), row)
        attn, k_out, v_out = pl.pallas_call(
            functools.partial(attention_kernel, heads),
            out_shape=(
                jax.ShapeDtypeStruct((batch_dev, steps * heads, head_dim), BF16),
                jax.ShapeDtypeStruct(k_loc.shape, BF16),
                jax.ShapeDtypeStruct(v_loc.shape, BF16),
            ),
            grid_spec=pltpu.PrefetchScalarGridSpec(
                num_scalar_prefetch=1,
                grid=(batch_dev,),
                in_specs=[
                    pl.BlockSpec((1, steps * heads, head_dim), row),
                    pl.BlockSpec((1, steps, head_dim), row),
                    pl.BlockSpec((1, steps, head_dim), row),
                    cache_spec,
                    cache_spec,
                ],
                out_specs=(pl.BlockSpec((1, steps * heads, head_dim), row), cache_spec, cache_spec),
            ),
            compiler_params=pltpu.CompilerParams(vmem_limit_bytes=KERNEL_VMEM),
            cost_estimate=pl.CostEstimate(flops=1_000_000_000, bytes_accessed=34_000_000, transcendentals=0),
            name="attention",
        )(own_lens, q_rot, k_new, v_new, k_loc, v_loc)

        attn_send = attn.reshape(batch_dev, steps, NDEV, attn_dev).transpose(2, 1, 0, 3).reshape(NDEV, PIECES, ROWS, attn_dev)
        next_rows = next_ids.reshape(pair_dims).transpose(0, 2, 1, 3).reshape(PIECES, piece_rows)
        log_probs = pl.pallas_call(
            functools.partial(back_kernel, vocab_dev, width, attn_dev, ff_dev, width ** -0.5),
            out_shape=jax.ShapeDtypeStruct((PIECES, piece_rows), F32),
            in_specs=[vmem, vmem, vmem, vmem, vmem, anym, anym],
            out_specs=vmem,
            scratch_shapes=[
                pltpu.VMEM((vocab_dev, width), BF16),
                pltpu.VMEM((out_dev, width), BF16),
                pltpu.VMEM((PIECES, NDEV, ROWS, attn_dev), BF16),
                pltpu.VMEM((PIECES, 8, 8, piece_rows), F32),
                pltpu.VMEM((PIECES, NZ, 8, piece_rows), F32),
                dma((2,)),
                dma((NDEV,)),
                dma((NDEV,)),
                dma((PIECES, 12)),
                dma((PIECES, 12)),
            ] + exchange,
            compiler_params=pltpu.CompilerParams(collective_id=1, has_side_effects=True, vmem_limit_bytes=KERNEL_VMEM),
            cost_estimate=pl.CostEstimate(flops=40_000_000_000, bytes_accessed=8_000_000, transcendentals=0),
            name="back",
        )(attn_send, mlp, x_own, final_gain.reshape(1, width), next_rows, w_out_loc, embed_loc)
        log_probs = log_probs.reshape(steps, HALVES, NDEV, ROWS).transpose(0, 2, 1, 3).reshape(steps, batch)
        return log_probs, k_out, v_out

    cache_spec = P('tp', None, None)
    return jax.shard_map(device_fn, mesh=mesh, in_specs=(P(), P(), P(), P('tp', None), P(), P(None, 'tp'), P('tp', None), P(), cache_spec, cache_spec), out_specs=(P(), cache_spec, cache_spec), check_vma=False)
```

time: 193 us -> 178 us (0.922)
  Pallas kernels: 176 us -> 165 us
  local copies, waits for them, and re-layouts: 15.6 us -> 8.75 us
    pallas_call x1, Pallas kernels: 87.9 us -> 76.7 us  [device_fn(): pl.pallas_call(functools.partial(back_kernel, vocab_dev, width, attn_dev,...]
    unnamed x10 -> x6, local copies, waits for them, and re-layouts: 9.57 us -> 0.01 us
    pallas_call x1, Pallas kernels: 12.7 us -> 20.4 us  [device_fn(): pl.pallas_call(functools.partial(attention_kernel, heads), out_shape=(jax...]
    pallas_call x1, Pallas kernels: 75 us -> 67.7 us  [device_fn(): pl.pallas_call(functools.partial(front_kernel, vocab_dev, width, qkv_dev,...]
    reshape x2 -> x6, local copies, waits for them, and re-layouts: 1.11 us -> 3.91 us  [the longest x2 1.57 us: device_fn(): qkv_parts.reshape(NDEV, steps, batch_dev, qkv_dev).transpose(1, 2, 0, 3)]
where the time goes in v2:
time: 178 us; the launch traced here: 177 us
  Pallas kernels  165 us (93%)
  local copies, waits for them, and re-layouts  8.75 us (5%)
  other arithmetic  2.78 us (2%)
    pallas_call x1, Pallas kernels, device_fn(): pl.pallas_call(functools.partial(back_kernel, vocab_dev, width, attn_dev,...  76.7 us
    pallas_call x1, Pallas kernels, device_fn(): pl.pallas_call(functools.partial(front_kernel, vocab_dev, width, qkv_dev,...  67.7 us
    pallas_call x1, Pallas kernels, device_fn(): pl.pallas_call(functools.partial(attention_kernel, heads), out_shape=(jax...  20.4 us

profile of v2, /device:TPU:0, one launch (start us, length us, event | category | flops | bytes accessed | tf_op | source)
XLA Modules:
  0.0 177.0 jit_solution(5956984932428875447)
XLA Ops:
  0.6 0.8 dynamic_slice.3.lens_ref
  1.4 0.0 copy-start.2
  1.4 0.1 add_convert_fusion.1
  1.5 1.3 reshape.105.gain_ref
  2.8 67.7 %front.1 = (bf16[4,8,2048]{2,1,0:T(8,128)(2,1)}, bf16[32,4,8,72]{3,2,1,0:T(8,128)(2,1)}, bf16[4,256,256]{2,1,0:T(8,128)(2,1)}) custom-call(s32[2,512]{1,0:T(2,128)} %tok_ref.1, bf16[1,2048]{1,0:T(2,128)(2,1)} %reshape.105.gain_ref, bf16[1536,2048]{1,0:T(8,128)(2,1)} %embed_ref.3, bf16[584,2048]{1,0:T(8,128)(2,1)} %bitcast.31), custom_call_target="tpu_custom_call" | custom-call | flops 40000000000 | bytes 8000000 | tf_op jit(solution)/shard_map/front/pallas_call | solution.py:485
  70.4 0.0 copy-done.2
  70.4 1.1 copy.27
  71.5 0.5 reshape.107
  72.0 0.6 slice_bitcast_fusion
  72.6 0.3 subtract_convert_fusion
  73.0 0.1 slice_convert_fusion
  73.1 0.2 reshape.116
  73.3 0.2 multiply_subtract_fusion
  73.5 0.8 fusion
  74.3 0.7 maximum_bitcast_fusion.kn_ref
  75.0 0.0 copy-start
  75.0 0.0 copy-start.1
  75.0 20.4 %attention.1 = (bf16[16,32,128]{2,1,0:T(8,128)(2,1)}, bf16[16,2048,128]{2,1,0:T(8,128)(2,1)}, bf16[16,2048,128]{2,1,0:T(8,128)(2,1)}) custom-call(s32[16]{0:T(128)} %copy-done.2, bf16[16,32,128]{2,1,0:T(8,128)(2,1)} %bitcast.26, bf16[16,2,128]{2,1,0:T(2,128)(2,1)} %maximum_bitcast_fusion.kn_ref, bf16[16,2,128]{2,1,0:T(2,128)(2,1)} %get-tuple-element.17.vn_ref, ...), custom_call_target="tpu_custom_call" | custom-call | flops 1000000000 | bytes 34000000 | tf_op jit(solution)/shard_map/attention/pallas_call | solution.py:524
  95.4 1.0 reshape.109
  96.5 0.9 copy.23
  97.3 0.0 copy-done
  97.3 0.2 reshape.112
  97.5 0.7 reshape.113.next_ref
  98.2 0.0 copy-done.1
  98.2 0.6 reshape.111.gain_ref
  98.8 76.7 %back.1 = f32[4,256]{1,0:T(4,128)} custom-call(bf16[32,4,8,64]{3,2,1,0:T(8,128)(2,1)} %bitcast.27, bf16[4,256,256]{2,1,0:T(8,128)(2,1)} %get-tuple-element.11.mlp_ref, bf16[4,8,2048]{2,1,0:T(8,128)(2,1)} %get-tuple-element.12.x_ref, bf16[1,2048]{1,0:T(2,128)(2,1)} %reshape.111.gain_ref, s32[4,256]{1,0:T(4,128)} %reshape.113.next_ref, ...), custom_call_target="tpu_custom_call" | custom-call | flops 40000000000 | bytes 8000000 | tf_op jit(solution)/shard_map/back/pallas_call | solution.py:550
  175.5 0.8 reshape.114
  176.3 0.1 copy.25
  176.3 0.7 reshape.115
  (2 shorter events, 0.0 us)
Async XLA Ops:
  1.4 69.0 %copy-start.2 = (s32[16]{0:T(128)}, s32[16]{0:T(128)S(1)}, u32[]{:S(2)}) copy-start(s32[16]{0:T(128)S(1)} %dynamic_slice.3.lens_ref) | copy-start | bytes 196
  75.0 22.4 %copy-start = (s32[2,512]{1,0:T(2,128)S(1)}, s32[2,512]{1,0:T(2,128)}, u32[]{:S(2)}) copy-start(s32[2,512]{1,0:T(2,128)} %param.11) | copy-start | bytes 12292
  75.0 23.2 %copy-start.1 = (bf16[2048]{0:T(1024)(128)(2,1)S(1)}, bf16[2048]{0:T(1024)(128)(2,1)}, u32[]{:S(2)}) copy-start(bf16[2048]{0:T(1024)(128)(2,1)} %param.17) | copy-start | bytes 12292

commit v3 on v2

--- a/solution.py
+++ b/solution.py
@@ -11,33 +11,27 @@
 NORM_EPS = 1e-6
 MESH_ID = pl.DeviceIdType.MESH
 ROWS = 8
+LANES = 128
 NZ = 4
 NDEV = 32
 STEPS = 2
 HALVES = 2
 PIECES = STEPS * HALVES
 FRONT_ORDER = (
-    "r00 r10 r01 r11 r20 r30 r02 r12 r21 r03 r13 r31 r04 r22 g00 r14 g10 r32 r23 g01 "
-    "r33 g11 r24 g20 g12 g02 r34 g30 g21 g03 g31 g13 g22 g32 g04 g14 g23 g24 g33 g34"
+    "r00", "r10", "r01", "r11", "r20", "r30", "r02", "r12", "r21", "r03",
+    "r13", "r31", "r04", "r22", "g00", "r14", "g10", "r32", "r23", "g01",
+    "r33", "g11", "r24", "g20", "g12", "g02", "r34", "g30", "g21", "g03",
+    "g31", "g13", "g22", "g32", "g04", "g14", "g23", "g24", "g33", "g34",
 )
 BACK_ORDER = (
-    "r00 r01 r10 r11 r20 r30 r02 r12 r21 r31 r03 r13 r04 g00 r32 r14 g10 r22 r33 g01 "
-    "g11 r23 g02 r34 g30 r24 g20 g12 g03 g31 g21 g13 g32 g04 g22 g33 g14 g23 g34 g24"
+    "r00", "r01", "r10", "r11", "r20", "r30", "r02", "r12", "r21", "r31",
+    "r03", "r13", "r04", "g00", "r32", "r14", "g10", "r22", "r33", "g01",
+    "g11", "r23", "g02", "r34", "g30", "r24", "g20", "g12", "g03", "g31",
+    "g21", "g13", "g32", "g04", "g22", "g33", "g14", "g23", "g34", "g24",
 )
 KERNEL_VMEM = 60 * 1024 * 1024
 BF16 = jnp.bfloat16
 F32 = jnp.float32
-
-
-def rotary(vectors, positions):
-    half_dim = vectors.shape[-1] // 2
-    inv_freq = ROPE_BASE ** (-jnp.arange(half_dim, dtype=jnp.float32) / half_dim)
-    angles = positions.astype(jnp.float32)[..., None] * inv_freq
-    cosine = jnp.cos(angles)
-    sine_val = jnp.sin(angles)
-    first_half = vectors[..., :half_dim]
-    second_half = vectors[..., half_dim:]
-    return jnp.concatenate([first_half * cosine - second_half * sine_val, second_half * cosine + first_half * sine_val], axis=-1)
 
 
 def norm_rows(values, gain):
@@ -216,7 +210,7 @@
         return [st0, st1, st2, st3, st4]
 
     stages = {"r": [rs_stages(n) for n in range(PIECES)], "g": [ag_stages(n) for n in range(PIECES)]}
-    for item in order.split():
+    for item in order:
         with jax.named_scope(item):
             stages[item[0]][int(item[1])][int(item[2])]()
     for cp in sent:
@@ -236,11 +230,12 @@
     for h in range(width // tile):
         cols = pl.ds(h * tile, tile)
         loads.append(pltpu.make_async_copy(embed_ref.at[:, cols], emb.at[:, cols], local_sem.at[h]))
-    pieces = ((wq, 0, qkv_dev), (wg, qkv_dev, ff_dev), (wu, qkv_dev + ff_dev, ff_dev))
+    pieces = ((wq.at[pl.ds(0, qkv_dev), :], 0, qkv_dev), (wg, qkv_dev, ff_dev), (wu, qkv_dev + ff_dev, ff_dev))
     for i, (dst, start, size) in enumerate(pieces):
         loads.append(pltpu.make_async_copy(w_ref.at[pl.ds(start, size), :], dst, local_sem.at[width // tile + i]))
     for cp in loads:
         cp.start()
+    wq[qkv_dev:, :] = jnp.zeros((LANES - qkv_dev, width), BF16)
     vocab_start = me * vocab_dev
     for s in range(STEPS):
         row = jnp.broadcast_to((tok_ref[s:s + 1, :] - vocab_start).astype(F32), (8, batch))
@@ -268,7 +263,7 @@
 
     def finalize(n, rows):
         x_ref[n] = rows.astype(BF16)
-        return norm_rows(rows, gain_ref[...].astype(F32))
+        return norm_rows(rows, gain_ref[...].astype(F32).reshape(1, width))
 
     def send_qkv(s, k):
         to = place.peer(k)
@@ -280,7 +275,7 @@
             for cp in loads[width // tile:]:
                 cp.wait()
         qkv = dot_nt(b["rows"][...], wq[...])
-        sq[n] = qkv.reshape(NDEV, ROWS, qkv_dev).astype(BF16)
+        sq[n] = qkv.reshape(NDEV, ROWS, LANES).astype(BF16)
         rq[me, n] = sq[n, me]
         if n % HALVES == HALVES - 1:
             def send(k, _):
@@ -312,25 +307,27 @@
 
 
 def back_kernel(vocab_dev, width, attn_dev, ff_dev, scale, send_ref, mlp_ref, x_ref, gain_ref, next_ref, w_ref, embed_ref, out_ref,
-                emb, wv, ac, r8, r4, local_sem, a_s, a_r, st_s, st_r, *bufs):
+                emb, wa, wv, ac, r8, r4, local_sem, a_s, a_r, st_s, st_r, *bufs):
     b = dict(zip(EXCHANGE_NAMES, bufs))
     place = Place()
     me = place.me
     r8[...] = jnp.zeros_like(r8)
     r4[...] = jnp.zeros_like(r4)
     barrier = greet(place)
-    load_w = pltpu.make_async_copy(w_ref, wv, local_sem.at[0])
-    load_e = pltpu.make_async_copy(embed_ref, emb, local_sem.at[1])
-    load_w.start()
+    load_w = []
+    for i, (start, size, dst) in enumerate(((0, attn_dev, wa.at[pl.ds(0, attn_dev), :]), (0, attn_dev, wa.at[pl.ds(attn_dev, attn_dev), :]), (attn_dev, ff_dev, wv))):
+        load_w.append(pltpu.make_async_copy(w_ref.at[pl.ds(start, size), :], dst, local_sem.at[i]))
+        load_w[-1].start()
+    load_e = pltpu.make_async_copy(embed_ref, emb, local_sem.at[3])
     load_e.start()
     vocab_start = me * vocab_dev
     total = NDEV * ROWS
 
     def send_attn(k):
         to = place.peer(k)
-        return remote(send_ref.at[to], ac.at[:, me], a_s.at[k], a_r.at[k], to)
-
-    ac[:, me] = send_ref[me]
+        return remote(send_ref.at[to], ac.at[me], a_s.at[k], a_r.at[k], to)
+
+    ac[me] = send_ref[me]
     with jax.named_scope("barrier"):
         pl.semaphore_wait(barrier, NDEV - 1)
 
@@ -340,7 +337,8 @@
 
     with jax.named_scope("attn_send"):
         lax.fori_loop(1, NDEV, send, 0)
-        load_w.wait()
+        for cp in load_w:
+            cp.wait()
 
     def arrive(k, _):
         send_attn(k).wait_recv()
@@ -351,12 +349,14 @@
 
     def produce(n):
         tile = 512
-        att = ac[n].astype(F32).reshape(total, attn_dev).astype(BF16)
+        att = ac[:, n % HALVES * ROWS:(n % HALVES + 1) * ROWS, :].astype(F32).reshape(total, LANES).astype(BF16)
+        own = lax.broadcasted_iota(jnp.int32, (total, LANES), 1) // attn_dev == n // HALVES
+        att = jnp.where(own, att, jnp.zeros_like(att))
 
         def mul(i, _):
             cols = pl.ds(pl.multiple_of(i * tile, tile), tile)
-            out = jnp.dot(att, wv[0:attn_dev, cols], preferred_element_type=F32)
-            out = out + jnp.dot(mlp_ref[n], wv[attn_dev:attn_dev + ff_dev, cols], preferred_element_type=F32)
+            out = jnp.dot(att, wa[:, cols], preferred_element_type=F32)
+            out = out + jnp.dot(mlp_ref[n], wv[:, cols], preferred_element_type=F32)
             b["part"][n, :, :, :, :, :, cols] = out.reshape(NZ, 2, 2, 2, ROWS, tile).astype(BF16)
             return 0
 
@@ -364,7 +364,7 @@
 
     def finalize(n, rows):
         resid = x_ref[n].astype(F32) + rows.astype(BF16).astype(F32)
-        return norm_rows(resid, gain_ref[...].astype(F32))
+        return norm_rows(resid, gain_ref[...].astype(F32).reshape(1, width))
 
     plane = lax.rem(me, 8)
 
@@ -411,7 +411,7 @@
         return top, den, hit
 
     run_exchange(place, b, width, BACK_ORDER, produce, lambda: None, finalize, consume)
-    last = [int(item[1]) for item in BACK_ORDER.split() if item[0] == "g" and item[2] == "4"]
+    last = [int(item[1]) for item in BACK_ORDER if item[0] == "g" and item[2] == "4"]
     for n in last:
         with jax.named_scope("plane"):
             for k in range(1, 8):
@@ -441,23 +441,92 @@
     lax.fori_loop(1, NDEV, finish, 0)
 
 
-def attention_kernel(heads, lens_ref, q_ref, kn_ref, vn_ref, kc_ref, vc_ref, o_ref, ko_ref, vo_ref):
-    first = lens_ref[pl.program_id(0)]
-    ko_ref[...] = kc_ref[...]
-    vo_ref[...] = vc_ref[...]
-    for s in range(STEPS):
-        pos = first + s
-        base = pl.multiple_of(lax.div(pos, 16) * 16, 16)
-        rows = lax.broadcasted_iota(jnp.int32, (16, ko_ref.shape[2]), 0) == pos - base
-        ko_ref[0, pl.ds(base, 16), :] = jnp.where(rows, kn_ref[0, s:s + 1, :], ko_ref[0, pl.ds(base, 16), :])
-        vo_ref[0, pl.ds(base, 16), :] = jnp.where(rows, vn_ref[0, s:s + 1, :], vo_ref[0, pl.ds(base, 16), :])
-    scores = dot_nt(q_ref[0], ko_ref[0])
-    times = lax.broadcasted_iota(jnp.int32, scores.shape, 1)
-    limit = first + jnp.where(lax.broadcasted_iota(jnp.int32, scores.shape, 0) >= heads, 1, 0)
-    scores = jnp.where(times <= limit, scores, -jnp.inf)
-    scores = jnp.exp(scores - jnp.max(scores, axis=1, keepdims=True))
-    probs = (scores / jnp.sum(scores, axis=1, keepdims=True)).astype(BF16)
-    o_ref[0] = jnp.dot(probs, vo_ref[0], preferred_element_type=F32).astype(BF16)
+def attention_kernel(heads, part_dev, lens_ref, qkv_ref, cos_ref, sin_ref, kc_ref, vc_ref, send_ref, ko_ref, vo_ref,
+                     kbuf, vbuf, qry, knew, vnew, att, in_sem, out_sem):
+    count, cache_len, head_dim = kc_ref.shape
+    rows = STEPS * count
+    ahead, group = 4, 2
+
+    def load(i):
+        return (pltpu.make_async_copy(kc_ref.at[i], kbuf.at[i], in_sem.at[0, i]),
+                pltpu.make_async_copy(vc_ref.at[i], vbuf.at[i], in_sem.at[1, i]))
+
+    def store(i):
+        return (pltpu.make_async_copy(kbuf.at[i], ko_ref.at[i], out_sem.at[0, i]),
+                pltpu.make_async_copy(vbuf.at[i], vo_ref.at[i], out_sem.at[1, i]))
+
+    for i in range(ahead):
+        for cp in load(i):
+            cp.start()
+    cosine, sine = cos_ref[...], sin_ref[...]
+    parts = [qkv_ref[j].astype(F32).reshape(rows, LANES)[:, :part_dev] for j in range(NDEV)]
+    for h in range(heads + 2):
+        lo, hi = h * head_dim, (h + 1) * head_dim
+        held = []
+        for j in range(lo // part_dev, (hi - 1) // part_dev + 1):
+            start, stop = max(lo, j * part_dev) - j * part_dev, min(hi, (j + 1) * part_dev) - j * part_dev
+            held.append(parts[j][:, start:stop])
+        vec = jnp.concatenate(held, axis=1)
+        if h <= heads:
+            vec = vec * cosine + pltpu.roll(vec, head_dim // 2, 1) * sine
+        if h < heads:
+            vec = vec * head_dim ** -0.5
+            for s in range(STEPS):
+                qry[pl.ds(s * heads + h, count, stride=STEPS * heads), :] = vec[s * count:(s + 1) * count]
+        elif h == heads:
+            knew[...] = vec
+        else:
+            vnew[...] = vec
+
+    def one(i):
+        first = lens_ref[i]
+        for s in range(STEPS):
+            pos = first + s
+            base = pl.multiple_of(lax.div(pos, 16) * 16, 16)
+            here = lax.broadcasted_iota(jnp.int32, (16, head_dim), 0) == pos - base
+            for buf, new in ((kbuf, knew), (vbuf, vnew)):
+                line = new[pl.ds(s * count + i, 1), :].astype(BF16)
+                buf[i, pl.ds(base, 16), :] = jnp.where(here, line, buf[i, pl.ds(base, 16), :])
+        query = qry[pl.ds(pl.multiple_of(i * STEPS * heads, STEPS * heads), STEPS * heads), :].astype(BF16)
+        scores = dot_nt(query, kbuf[i])
+        times = lax.broadcasted_iota(jnp.int32, scores.shape, 1)
+        limit = first + jnp.where(lax.broadcasted_iota(jnp.int32, (STEPS * heads, 1), 0) >= heads, 1, 0)
+        scores = jnp.where(times <= limit, scores, -jnp.inf)
+        scores = jnp.exp(scores - jnp.max(scores, axis=1, keepdims=True))
+        probs = (scores * (1.0 / jnp.sum(scores, axis=1, keepdims=True))).astype(BF16)
+        out = jnp.dot(probs, vbuf[i], preferred_element_type=F32)
+        old, new = out[:heads], out[heads:]
+        low = lax.broadcasted_iota(jnp.int32, old.shape, 1) < head_dim // 2
+        att[pl.ds(i, heads, stride=2 * count), :] = jnp.where(low, old, pltpu.roll(new, head_dim // 2, 1))
+        att[pl.ds(count + i, heads, stride=2 * count), :] = jnp.where(low, pltpu.roll(old, head_dim // 2, 1), new)
+
+    def body(g, _):
+        for u in range(group):
+            for cp in load(g * group + u):
+                cp.wait()
+
+        @pl.when(g < (count - ahead) // group)
+        def _():
+            for u in range(group):
+                for cp in load(g * group + u + ahead):
+                    cp.start()
+
+        for u in range(group):
+            one(g * group + u)
+        for u in range(group):
+            for cp in store(g * group + u):
+                cp.start()
+        return 0
+
+    lax.fori_loop(0, count // group, body, 0)
+    send_ref[...] = att[...].reshape(NDEV, count, LANES).astype(BF16)
+
+    def drain(i, _):
+        for cp in store(i):
+            cp.wait()
+        return 0
+
+    lax.fori_loop(0, count, drain, 0)
 
 
 def solution(mesh):
@@ -486,7 +555,7 @@
             functools.partial(front_kernel, vocab_dev, width, qkv_dev, ff_dev),
             out_shape=(
                 jax.ShapeDtypeStruct((PIECES, ROWS, width), BF16),
-                jax.ShapeDtypeStruct((NDEV, PIECES, ROWS, qkv_dev), BF16),
+                jax.ShapeDtypeStruct((NDEV, PIECES, ROWS, LANES), BF16),
                 jax.ShapeDtypeStruct((PIECES, piece_rows, ff_dev), BF16),
             ),
             in_specs=[vmem, vmem, anym, anym],
@@ -495,11 +564,11 @@
                 pltpu.VMEM((vocab_dev, width), BF16),
                 pltpu.VMEM((steps, NDEV, HALVES, ROWS, 8), jnp.int32),
                 pltpu.VMEM((piece_rows, vocab_dev), BF16),
-                pltpu.VMEM((qkv_dev, width), BF16),
+                pltpu.VMEM((LANES, width), BF16),
                 pltpu.VMEM((ff_dev, width), BF16),
                 pltpu.VMEM((ff_dev, width), BF16),
-                pltpu.VMEM((PIECES, NDEV, ROWS, qkv_dev), BF16),
-                pltpu.VMEM((NDEV, PIECES, ROWS, qkv_dev), BF16),
+                pltpu.VMEM((PIECES, NDEV, ROWS, LANES), BF16),
+                pltpu.VMEM((NDEV, PIECES, ROWS, LANES), BF16),
                 dma((8,)),
                 dma((steps, NDEV)),
                 dma((steps, NDEV)),
@@ -507,45 +576,39 @@
             compiler_params=pltpu.CompilerParams(collective_id=0, has_side_effects=True, vmem_limit_bytes=KERNEL_VMEM),
             cost_estimate=pl.CostEstimate(flops=40_000_000_000, bytes_accessed=8_000_000, transcendentals=0),
             name="front",
-        )(tok_ids, ln_gain.reshape(1, width), embed_loc, w_in_loc.T)
-
-        qkv_own = qkv_parts.reshape(NDEV, steps, batch_dev, qkv_dev).transpose(1, 2, 0, 3).reshape(steps, batch_dev, NDEV * qkv_dev)
+        )(tok_ids, ln_gain, embed_loc, w_in_loc.T)
+
+        half_dim = head_dim // 2
+        inv_freq = ROPE_BASE ** (-jnp.arange(half_dim, dtype=jnp.float32) / half_dim)
         positions = own_lens[None, :] + jnp.arange(steps, dtype=own_lens.dtype)[:, None]
-        queries = qkv_own[..., :attn_width].reshape(steps, batch_dev, heads, head_dim).astype(F32)
-        q_rot = (rotary(queries, positions[..., None]) * head_dim ** -0.5).astype(BF16)
-        q_rot = q_rot.transpose(1, 0, 2, 3).reshape(batch_dev, steps * heads, head_dim)
-        k_new = rotary(qkv_own[..., attn_width:attn_width + head_dim].astype(F32), positions).astype(BF16).transpose(1, 0, 2)
-        v_new = qkv_own[..., attn_width + head_dim:].transpose(1, 0, 2)
-
-        def row(i, lens):
-            return (i, 0, 0)
-
-        cache_spec = pl.BlockSpec((1, cache_len, head_dim), row)
-        attn, k_out, v_out = pl.pallas_call(
-            functools.partial(attention_kernel, heads),
+        angles = positions.reshape(-1, 1).astype(F32) * jnp.concatenate([inv_freq, inv_freq])
+        sign = jnp.where(jnp.arange(head_dim) < half_dim, -1.0, 1.0)
+        cosine, sine = jnp.cos(angles), jnp.sin(angles) * sign
+        smem = pl.BlockSpec(memory_space=pltpu.SMEM)
+        attn_send, k_out, v_out = pl.pallas_call(
+            functools.partial(attention_kernel, heads, qkv_dev),
             out_shape=(
-                jax.ShapeDtypeStruct((batch_dev, steps * heads, head_dim), BF16),
+                jax.ShapeDtypeStruct((NDEV, batch_dev, LANES), BF16),
                 jax.ShapeDtypeStruct(k_loc.shape, BF16),
                 jax.ShapeDtypeStruct(v_loc.shape, BF16),
             ),
-            grid_spec=pltpu.PrefetchScalarGridSpec(
-                num_scalar_prefetch=1,
-                grid=(batch_dev,),
-                in_specs=[
-                    pl.BlockSpec((1, steps * heads, head_dim), row),
-                    pl.BlockSpec((1, steps, head_dim), row),
-                    pl.BlockSpec((1, steps, head_dim), row),
-                    cache_spec,
-                    cache_spec,
-                ],
-                out_specs=(pl.BlockSpec((1, steps * heads, head_dim), row), cache_spec, cache_spec),
-            ),
+            in_specs=[smem, vmem, vmem, vmem, anym, anym],
+            out_specs=(vmem, anym, anym),
+            scratch_shapes=[
+                pltpu.VMEM(k_loc.shape, BF16),
+                pltpu.VMEM(v_loc.shape, BF16),
+                pltpu.VMEM((batch_dev * steps * heads, head_dim), F32),
+                pltpu.VMEM((steps * batch_dev, head_dim), F32),
+                pltpu.VMEM((steps * batch_dev, head_dim), F32),
+                pltpu.VMEM((NDEV * batch_dev, LANES), F32),
+                dma((2, batch_dev)),
+                dma((2, batch_dev)),
+            ],
             compiler_params=pltpu.CompilerParams(vmem_limit_bytes=KERNEL_VMEM),
             cost_estimate=pl.CostEstimate(flops=1_000_000_000, bytes_accessed=34_000_000, transcendentals=0),
             name="attention",
-        )(own_lens, q_rot, k_new, v_new, k_loc, v_loc)
-
-        attn_send = attn.reshape(batch_dev, steps, NDEV, attn_dev).transpose(2, 1, 0, 3).reshape(NDEV, PIECES, ROWS, attn_dev)
+        )(own_lens, qkv_parts, cosine, sine, k_loc, v_loc)
+
         next_rows = next_ids.reshape(pair_dims).transpose(0, 2, 1, 3).reshape(PIECES, piece_rows)
         log_probs = pl.pallas_call(
             functools.partial(back_kernel, vocab_dev, width, attn_dev, ff_dev, width ** -0.5),
@@ -554,11 +617,12 @@
             out_specs=vmem,
             scratch_shapes=[
                 pltpu.VMEM((vocab_dev, width), BF16),
-                pltpu.VMEM((out_dev, width), BF16),
-                pltpu.VMEM((PIECES, NDEV, ROWS, attn_dev), BF16),
+                pltpu.VMEM((2 * attn_dev, width), BF16),
+                pltpu.VMEM((ff_dev, width), BF16),
+                pltpu.VMEM((NDEV, batch_dev, LANES), BF16),
                 pltpu.VMEM((PIECES, 8, 8, piece_rows), F32),
                 pltpu.VMEM((PIECES, NZ, 8, piece_rows), F32),
-                dma((2,)),
+                dma((4,)),
                 dma((NDEV,)),
                 dma((NDEV,)),
                 dma((PIECES, 12)),
@@ -567,7 +631,7 @@
             compiler_params=pltpu.CompilerParams(collective_id=1, has_side_effects=True, vmem_limit_bytes=KERNEL_VMEM),
             cost_estimate=pl.CostEstimate(flops=40_000_000_000, bytes_accessed=8_000_000, transcendentals=0),
             name="back",
-        )(attn_send, mlp, x_own, final_gain.reshape(1, width), next_rows, w_out_loc, embed_loc)
+        )(attn_send, mlp, x_own, final_gain, next_rows, w_out_loc, embed_loc)
         log_probs = log_probs.reshape(steps, HALVES, NDEV, ROWS).transpose(0, 2, 1, 3).reshape(steps, batch)
         return log_probs, k_out, v_out
 

time: 178 us -> 162 us (0.910)
  Pallas kernels: 165 us -> 157 us
  local copies, waits for them, and re-layouts: 8.75 us -> 3.24 us
  other arithmetic: 2.78 us -> 0.85 us
    pallas_call x1, Pallas kernels: 20.4 us -> 14.5 us  [device_fn(): pl.pallas_call(functools.partial(attention_kernel, heads, qkv_dev), out_s...]
    reshape x6 -> x0, local copies, waits for them, and re-layouts: 5.37 us -> none  [the longest x2 1.91 us: device_fn(): attn.reshape(batch_dev, steps, NDEV, attn_dev).transpose(2, 1, 0, 3)]
    pallas_call x1, Pallas kernels: 76.7 us -> 74.7 us  [device_fn(): pl.pallas_call(functools.partial(back_kernel, vocab_dev, width, attn_dev,...]
where the time goes in v3:
time: 162 us
  Pallas kernels  157 us (97%)
  local copies, waits for them, and re-layouts  3.24 us (2%)
    pallas_call x1, Pallas kernels, device_fn(): pl.pallas_call(functools.partial(back_kernel, vocab_dev, width, attn_dev,...  74.7 us
    pallas_call x1, Pallas kernels, device_fn(): pl.pallas_call(functools.partial(front_kernel, vocab_dev, width, qkv_dev,...  67.5 us
    pallas_call x1, Pallas kernels, device_fn(): pl.pallas_call(functools.partial(attention_kernel, heads, qkv_dev), out_s...  14.5 us

profile of v3, /device:TPU:0, one launch (start us, length us, event | category | flops | bytes accessed | tf_op | source)
XLA Modules:
  0.0 161.6 jit_solution(3947532840587183232)
XLA Ops:
  0.6 0.8 dynamic_slice.3.lens_ref
  1.4 0.0 copy-start.1
  1.4 0.1 convert_element_type.12
  1.5 0.1 compare_select_fusion
  1.6 0.8 fusion
  2.3 67.5 %front.1 = (bf16[4,8,2048]{2,1,0:T(8,128)(2,1)}, bf16[32,4,8,128]{3,2,1,0:T(8,128)(2,1)}, bf16[4,256,256]{2,1,0:T(8,128)(2,1)}) custom-call(s32[2,512]{1,0:T(2,128)} %tok_ref.1, bf16[2048]{0:T(1024)(128)(2,1)} %gain_ref.2, bf16[1536,2048]{1,0:T(8,128)(2,1)} %embed_ref.3, bf16[584,2048]{1,0:T(8,128)(2,1)} %bitcast.7), custom_call_target="tpu_custom_call" | custom-call | flops 40000000000 | bytes 8000000 | tf_op jit(solution)/shard_map/front/pallas_call | solution.py:554
  69.9 0.0 copy-done.1
  69.9 0.0 copy-start
  69.9 14.5 %attention.1 = (bf16[32,16,128]{2,1,0:T(8,128)(2,1)}, bf16[16,2048,128]{2,1,0:T(8,128)(2,1)}, bf16[16,2048,128]{2,1,0:T(8,128)(2,1)}) custom-call(s32[16]{0:T(128)} %copy-done.1, bf16[32,4,8,128]{3,2,1,0:T(8,128)(2,1)} %get-tuple-element.9.qkv_ref, f32[32,128]{1,0:T(8,128)} %get-tuple-element.16.cos_ref, f32[32,128]{1,0:T(8,128)} %get-tuple-element.15.sin_ref, ...), custom_call_target="tpu_custom_call" | custom-call | flops 1000000000 | bytes 34000000 | tf_op jit(solution)/shard_map/attention/pallas_call | solution.py:588
  84.4 0.0 copy-done
  84.4 0.2 reshape.42
  84.6 0.7 reshape.43.next_ref
  85.3 74.7 %back.1 = f32[4,256]{1,0:T(4,128)} custom-call(bf16[32,16,128]{2,1,0:T(8,128)(2,1)} %get-tuple-element.10.send_ref, bf16[4,256,256]{2,1,0:T(8,128)(2,1)} %get-tuple-element.11.mlp_ref, bf16[4,8,2048]{2,1,0:T(8,128)(2,1)} %get-tuple-element.12.x_ref, bf16[2048]{0:T(1024)(128)(2,1)} %gain_ref.3, s32[4,256]{1,0:T(4,128)} %reshape.43.next_ref, ...), custom_call_target="tpu_custom_call" | custom-call | flops 40000000000 | bytes 8000000 | tf_op jit(solution)/shard_map/back/pallas_call | solution.py:613
  160.0 0.8 reshape.44
  160.8 0.1 copy.16
  160.9 0.7 reshape.45
  (3 shorter events, 0.0 us)
Async XLA Ops:
  1.4 68.5 %copy-start.1 = (s32[16]{0:T(128)}, s32[16]{0:T(128)S(1)}, u32[]{:S(2)}) copy-start(s32[16]{0:T(128)S(1)} %dynamic_slice.3.lens_ref) | copy-start | bytes 196
  69.9 14.6 %copy-start = (s32[2,512]{1,0:T(2,128)S(1)}, s32[2,512]{1,0:T(2,128)}, u32[]{:S(2)}) copy-start(s32[2,512]{1,0:T(2,128)} %param.11) | copy-start | bytes 12292

commit v4 on v3

--- a/solution.py
+++ b/solution.py
@@ -17,18 +17,31 @@
 STEPS = 2
 HALVES = 2
 PIECES = STEPS * HALVES
+SPLIT = 2
 FRONT_ORDER = (
-    "r00", "r10", "r01", "r11", "r20", "r30", "r02", "r12", "r21", "r03",
-    "r13", "r31", "r04", "r22", "g00", "r14", "g10", "r32", "r23", "g01",
-    "r33", "g11", "r24", "g20", "g12", "g02", "r34", "g30", "g21", "g03",
-    "g31", "g13", "g22", "g32", "g04", "g14", "g23", "g24", "g33", "g34",
+    "r000", "r010", "r001", "r100", "r011", "r110", "r101", "r200", "r002", "r111",
+    "r012", "r210", "r300", "r102", "r003", "r310", "r112", "r201", "r013", "r211",
+    "r103", "r301", "r311", "r113", "r014", "r004", "g000", "g010", "r212", "r202",
+    "r302", "r114", "r104", "g100", "r312", "g001", "g110", "r213", "r203", "g101",
+    "r313", "g011", "r303", "g111", "g102", "g012", "r214", "r204", "g200", "g002",
+    "g210", "g112", "g013", "r304", "r314", "g300", "g310", "g201", "g211", "g003",
+    "g113", "g202", "g114", "g004", "g301", "g311", "g103", "g014", "g212", "c000",
+    "c001", "g302", "g312", "g203", "g104", "c100", "c101", "g204", "g303", "g213",
+    "g313", "g304", "t000", "g214", "c200", "g314", "c300", "t100", "c201", "c301",
 )
 BACK_ORDER = (
-    "r00", "r01", "r10", "r11", "r20", "r30", "r02", "r12", "r21", "r31",
-    "r03", "r13", "r04", "g00", "r32", "r14", "g10", "r22", "r33", "g01",
-    "g11", "r23", "g02", "r34", "g30", "r24", "g20", "g12", "g03", "g31",
-    "g21", "g13", "g32", "g04", "g22", "g33", "g14", "g23", "g34", "g24",
+    "r000", "r010", "r001", "r100", "r011", "r110", "r200", "r101", "r210", "r002",
+    "r012", "r111", "r300", "r310", "r102", "r201", "r003", "r211", "r013", "r112",
+    "r103", "r004", "r301", "r014", "g000", "r212", "g010", "r113", "r202", "g001",
+    "r311", "r104", "r213", "g011", "r203", "g002", "r302", "r114", "g100", "g110",
+    "g012", "r312", "r204", "r214", "g200", "g210", "g003", "g101", "g013", "g111",
+    "r313", "g004", "r303", "g102", "g014", "c000", "g201", "g112", "g211", "c001",
+    "c002", "g202", "g103", "r314", "r304", "g300", "g104", "g310", "g113", "g212",
+    "t000", "g114", "g301", "c100", "g311", "c101", "g213", "g302", "g203", "c102",
+    "g312", "g204", "g214", "c200", "c201", "t100", "g303", "g313", "c202", "g304",
+    "g314", "c300", "c301", "c302", "t200", "t001", "t300", "t101", "t201", "t301",
 )
+FRONT_FIRST, BACK_FIRST = 0, 0
 KERNEL_VMEM = 60 * 1024 * 1024
 BF16 = jnp.bfloat16
 F32 = jnp.float32
@@ -78,35 +91,36 @@
 
 
 def exchange_scratch(width):
-    half = width // 2
+    part = width // SPLIT
+    lead = (PIECES, SPLIT)
     return dict(
         part=pltpu.VMEM((PIECES, NZ, 2, 2, 2, ROWS, width), BF16),
         rc=pltpu.VMEM((PIECES, NZ, 2, 2, ROWS, width), BF16),
         s1=pltpu.VMEM((PIECES, NZ, 2, 2, ROWS, width), BF16),
-        r1a=pltpu.VMEM((PIECES, NZ, 2, ROWS, half), BF16),
-        r1b=pltpu.VMEM((PIECES, NZ, 2, ROWS, half), BF16),
-        s2a=pltpu.VMEM((PIECES, NZ, 2, ROWS, half), BF16),
-        s2b=pltpu.VMEM((PIECES, NZ, 2, ROWS, half), BF16),
-        r2a=pltpu.VMEM((PIECES, NZ, ROWS, half), BF16),
-        r2b=pltpu.VMEM((PIECES, NZ, ROWS, half), BF16),
+        r1a=pltpu.VMEM(lead + (NZ, 2, ROWS, part // 2), BF16),
+        r1b=pltpu.VMEM(lead + (NZ, 2, ROWS, part // 2), BF16),
+        s2a=pltpu.VMEM(lead + (NZ, 2, ROWS, part // 2), BF16),
+        s2b=pltpu.VMEM(lead + (NZ, 2, ROWS, part // 2), BF16),
+        r2a=pltpu.VMEM(lead + (NZ, ROWS, part // 2), BF16),
+        r2b=pltpu.VMEM(lead + (NZ, ROWS, part // 2), BF16),
         s3=pltpu.VMEM((PIECES, NZ, ROWS, width), BF16),
         r3=pltpu.VMEM((PIECES, NZ - 1, ROWS, width), BF16),
         full=pltpu.VMEM((PIECES, NZ, 2, 2, 2, ROWS, width), BF16),
-        rows=pltpu.VMEM((NDEV * ROWS, width), BF16),
-        rs_s=pltpu.SemaphoreType.DMA((PIECES, 8)),
-        rs_r=pltpu.SemaphoreType.DMA((PIECES, 8)),
-        ag_s=pltpu.SemaphoreType.DMA((PIECES, 8)),
-        ag_r=pltpu.SemaphoreType.DMA((PIECES, 8)),
+        rows=pltpu.VMEM((PIECES, NDEV * ROWS, width), BF16),
+        rs_s=pltpu.SemaphoreType.DMA((PIECES, SPLIT * 8)),
+        rs_r=pltpu.SemaphoreType.DMA((PIECES, SPLIT * 8)),
+        ag_s=pltpu.SemaphoreType.DMA((PIECES, SPLIT * 8)),
+        ag_r=pltpu.SemaphoreType.DMA((PIECES, SPLIT * 8)),
     )
 
 
 EXCHANGE_NAMES = ("part", "rc", "s1", "r1a", "r1b", "s2a", "s2b", "r2a", "r2b", "s3", "r3", "full", "rows", "rs_s", "rs_r", "ag_s", "ag_r")
 
 
-def run_exchange(place, b, width, order, produce, barrier_wait, finalize, consume):
+def run_exchange(place, b, width, order, produce, barrier_wait, finalize, consume, after):
     x, y, z, c = place.x, place.y, place.z, place.c
-    half = width // 2
-    ca, cb = pl.ds(0, half), pl.ds(half, half)
+    wide = width // SPLIT
+    half = wide // 2
     full = b["full"]
     sent = []
 
@@ -120,41 +134,43 @@
 
         lax.fori_loop(0, NZ, body, 0)
 
-    def rs_stages(n):
+    def rs_stages(n, h):
         live = {}
+        cols = pl.ds(h * wide, wide)
+        ca, cb = pl.ds(h * wide, half), pl.ds(h * wide + half, half)
 
         def go(j, src, dst, dev):
-            cp = remote(src, dst, b["rs_s"].at[n, j], b["rs_r"].at[n, j], dev)
+            cp = remote(src, dst, b["rs_s"].at[n, h * 8 + j], b["rs_r"].at[n, h * 8 + j], dev)
             cp.start()
             live[j] = cp
             sent.append(cp)
 
         def st0():
-            produce(n)
+            produce(n, h)
             barrier_wait()
-            go(0, b["part"].at[n, :, :, :, 1 - c], b["rc"].at[n], place.sib)
+            go(0, b["part"].at[n, :, :, :, 1 - c, :, cols], b["rc"].at[n, :, :, :, :, cols], place.sib)
 
         def st1():
             live[0].wait_recv()
-            add_z(lambda i: b["s1"].at[n, i], lambda i: b["part"].at[n, i, :, :, c], lambda i: b["rc"].at[n, i])
-            go(1, b["s1"].at[n, :, :, 1 - x, :, ca], b["r1a"].at[n], place.xpeer)
-            go(2, b["s1"].at[n, :, 1 - y, :, :, cb], b["r1b"].at[n], place.ypeer)
+            add_z(lambda i: b["s1"].at[n, i, :, :, :, cols], lambda i: b["part"].at[n, i, :, :, c, :, cols], lambda i: b["rc"].at[n, i, :, :, :, cols])
+            go(1, b["s1"].at[n, :, :, 1 - x, :, ca], b["r1a"].at[n, h], place.xpeer)
+            go(2, b["s1"].at[n, :, 1 - y, :, :, cb], b["r1b"].at[n, h], place.ypeer)
 
         def st2():
             live[1].wait_recv()
-            add_z(lambda i: b["s2a"].at[n, i], lambda i: b["s1"].at[n, i, :, x, :, ca], lambda i: b["r1a"].at[n, i])
-            go(3, b["s2a"].at[n, :, 1 - y], b["r2a"].at[n], place.ypeer)
+            add_z(lambda i: b["s2a"].at[n, h, i], lambda i: b["s1"].at[n, i, :, x, :, ca], lambda i: b["r1a"].at[n, h, i])
+            go(3, b["s2a"].at[n, h, :, 1 - y], b["r2a"].at[n, h], place.ypeer)
             live[2].wait_recv()
-            add_z(lambda i: b["s2b"].at[n, i], lambda i: b["s1"].at[n, i, y, :, :, cb], lambda i: b["r1b"].at[n, i])
-            go(4, b["s2b"].at[n, :, 1 - x], b["r2b"].at[n], place.xpeer)
+            add_z(lambda i: b["s2b"].at[n, h, i], lambda i: b["s1"].at[n, i, y, :, :, cb], lambda i: b["r1b"].at[n, h, i])
+            go(4, b["s2b"].at[n, h, :, 1 - x], b["r2b"].at[n, h], place.xpeer)
 
         def st3():
             live[3].wait_recv()
-            add(b["s3"].at[n, :, :, ca], b["s2a"].at[n, :, y], b["r2a"].at[n])
+            add(b["s3"].at[n, :, :, ca], b["s2a"].at[n, h, :, y], b["r2a"].at[n, h])
             live[4].wait_recv()
-            add(b["s3"].at[n, :, :, cb], b["s2b"].at[n, :, x], b["r2b"].at[n])
+            add(b["s3"].at[n, :, :, cb], b["s2b"].at[n, h, :, x], b["r2b"].at[n, h])
             for k in range(1, NZ):
-                go(4 + k, b["s3"].at[n, lax.rem(z + k, NZ)], b["r3"].at[n, k - 1], place.zpeer(k))
+                go(4 + k, b["s3"].at[n, lax.rem(z + k, NZ), :, cols], b["r3"].at[n, k - 1, :, cols], place.zpeer(k))
 
         def st4():
             for k in range(1, NZ):
@@ -162,22 +178,25 @@
 
         return [st0, st1, st2, st3, st4]
 
-    def ag_stages(n):
+    def ag_stages(n, h):
         live = {}
+        cols = pl.ds(h * wide, wide)
+        ca, cb = pl.ds(h * wide, half), pl.ds(h * wide + half, half)
 
         def go(j, ref, dev):
-            cp = remote(ref, ref, b["ag_s"].at[n, j], b["ag_r"].at[n, j], dev)
+            cp = remote(ref, ref, b["ag_s"].at[n, h * 8 + j], b["ag_r"].at[n, h * 8 + j], dev)
             cp.start()
             live[j] = cp
             sent.append(cp)
 
         def st0():
-            total = b["s3"][n, z].astype(F32)
+            if h == 0:
+                total = b["s3"][n, z].astype(F32)
+                for k in range(1, NZ):
+                    total = total + b["r3"][n, k - 1].astype(F32)
+                full[n, z, y, x, c] = finalize(n, total)
             for k in range(1, NZ):
-                total = total + b["r3"][n, k - 1].astype(F32)
-            full[n, z, y, x, c] = finalize(n, total)
-            for k in range(1, NZ):
-                go(k - 1, full.at[n, z, y, x, c], place.zpeer(k))
+                go(k - 1, full.at[n, z, y, x, c, :, cols], place.zpeer(k))
 
         def st1():
             for k in range(1, NZ):
@@ -194,25 +213,33 @@
         def st3():
             live[5].wait_recv()
             live[6].wait_recv()
-            go(7, full.at[n, :, :, :, c], place.sib)
+            go(7, full.at[n, :, :, :, c, :, cols], place.sib)
 
         def st4():
             live[7].wait_recv()
 
             def body(i, _):
-                block = full[n, i].astype(F32).reshape(8 * ROWS, width).astype(BF16)
-                b["rows"][pl.ds(pl.multiple_of(i * 8 * ROWS, 8 * ROWS), 8 * ROWS), :] = block
+                block = full[n, i, :, :, :, :, cols].astype(F32).reshape(8 * ROWS, wide).astype(BF16)
+                b["rows"][n, pl.ds(pl.multiple_of(i * 8 * ROWS, 8 * ROWS), 8 * ROWS), cols] = block
                 return 0
 
             lax.fori_loop(0, NZ, body, 0)
-            consume(n)
 
         return [st0, st1, st2, st3, st4]
 
-    stages = {"r": [rs_stages(n) for n in range(PIECES)], "g": [ag_stages(n) for n in range(PIECES)]}
+    scatter = [[rs_stages(n, h) for h in range(SPLIT)] for n in range(PIECES)]
+    gather = [[ag_stages(n, h) for h in range(SPLIT)] for n in range(PIECES)]
     for item in order:
+        kind, n, h, j = item[0], int(item[1]), int(item[2]), int(item[3])
         with jax.named_scope(item):
-            stages[item[0]][int(item[1])][int(item[2])]()
+            if kind == "r":
+                scatter[n][h][j]()
+            elif kind == "g":
+                gather[n][h][j]()
+            elif kind == "c":
+                consume(n, j)
+            else:
+                after(n, j)
     for cp in sent:
         cp.wait_send()
 
@@ -241,18 +268,22 @@
         row = jnp.broadcast_to((tok_ref[s:s + 1, :] - vocab_start).astype(F32), (8, batch))
         ids[s] = row.T.astype(jnp.int32).reshape(NDEV, HALVES, ROWS, 8)
 
-    def produce(n):
+    def produce(n, part):
+        if part == 0:
+            build(n)
+        for h in range(part * width // SPLIT // tile, (part + 1) * width // SPLIT // tile):
+            cols = pl.ds(h * tile, tile)
+            if n == 0:
+                loads[h].wait()
+            out = jnp.dot(hot[...], emb[:, cols], preferred_element_type=F32)
+            b["part"][n, :, :, :, :, :, cols] = out.reshape(NZ, 2, 2, 2, ROWS, tile).astype(BF16)
+
+    def build(n):
         col = ids[n // HALVES, :, n % HALVES].reshape(total, 8)
         for i in range(2):
             lanes = lax.broadcasted_iota(jnp.int32, (total // 2, vocab_dev), 1)
             mine = col[i * total // 2:(i + 1) * total // 2, 0:1]
             hot[pl.ds(i * total // 2, total // 2), :] = jnp.where(mine == lanes, 1.0, 0.0).astype(BF16)
-        for h in range(width // tile):
-            cols = pl.ds(h * tile, tile)
-            if n == 0:
-                loads[h].wait()
-            out = jnp.dot(hot[...], emb[:, cols], preferred_element_type=F32)
-            b["part"][n, :, :, :, :, :, cols] = out.reshape(NZ, 2, 2, 2, ROWS, tile).astype(BF16)
 
     pending = [True]
 
@@ -270,24 +301,28 @@
         pair = pl.ds(HALVES * s, HALVES)
         return remote(sq.at[pair, to], rq.at[me, pair], a_s.at[s, k], a_r.at[s, k], to)
 
-    def consume(n):
-        if n == 0:
+    def consume(n, j):
+        if n == FRONT_FIRST and j == 0:
             for cp in loads[width // tile:]:
                 cp.wait()
-        qkv = dot_nt(b["rows"][...], wq[...])
-        sq[n] = qkv.reshape(NDEV, ROWS, LANES).astype(BF16)
-        rq[me, n] = sq[n, me]
-        if n % HALVES == HALVES - 1:
-            def send(k, _):
-                send_qkv(n // HALVES, k).start()
-                return 0
-
-            lax.fori_loop(1, NDEV, send, 0)
-        gate = dot_nt(b["rows"][...], wg[...]).astype(BF16).astype(F32)
-        up = dot_nt(b["rows"][...], wu[...]).astype(BF16).astype(F32)
-        mlp_ref[n] = ((gate * (1.0 / (1.0 + jnp.exp(-gate)))) * up).astype(BF16)
-
-    run_exchange(place, b, width, FRONT_ORDER, produce, barrier_wait, finalize, consume)
+        hid = b["rows"].at[n]
+        if j == 0:
+            qkv = dot_nt(hid[...], wq[...])
+            sq[n] = qkv.reshape(NDEV, ROWS, LANES).astype(BF16)
+            rq[me, n] = sq[n, me]
+        else:
+            gate = dot_nt(hid[...], wg[...]).astype(BF16).astype(F32)
+            up = dot_nt(hid[...], wu[...]).astype(BF16).astype(F32)
+            mlp_ref[n] = ((gate * (1.0 / (1.0 + jnp.exp(-gate)))) * up).astype(BF16)
+
+    def after(s, _):
+        def send(k, _):
+            send_qkv(s, k).start()
+            return 0
+
+        lax.fori_loop(1, NDEV, send, 0)
+
+    run_exchange(place, b, width, FRONT_ORDER, produce, barrier_wait, finalize, consume, after)
     with jax.named_scope("qkv_arrive"):
         for s in range(STEPS):
             def finish(k, _):
@@ -307,7 +342,7 @@
 
 
 def back_kernel(vocab_dev, width, attn_dev, ff_dev, scale, send_ref, mlp_ref, x_ref, gain_ref, next_ref, w_ref, embed_ref, out_ref,
-                emb, wa, wv, ac, r8, r4, local_sem, a_s, a_r, st_s, st_r, *bufs):
+                emb, wa, wv, ac, run, r8, r4, local_sem, a_s, a_r, st_s, st_r, *bufs):
     b = dict(zip(EXCHANGE_NAMES, bufs))
     place = Place()
     me = place.me
@@ -347,20 +382,21 @@
     with jax.named_scope("attn_arrive"):
         lax.fori_loop(1, NDEV, arrive, 0)
 
-    def produce(n):
+    def produce(n, part):
         tile = 512
+        per = width // SPLIT // tile
         att = ac[:, n % HALVES * ROWS:(n % HALVES + 1) * ROWS, :].astype(F32).reshape(total, LANES).astype(BF16)
         own = lax.broadcasted_iota(jnp.int32, (total, LANES), 1) // attn_dev == n // HALVES
         att = jnp.where(own, att, jnp.zeros_like(att))
 
         def mul(i, _):
-            cols = pl.ds(pl.multiple_of(i * tile, tile), tile)
+            cols = pl.ds(pl.multiple_of((part * per + i) * tile, tile), tile)
             out = jnp.dot(att, wa[:, cols], preferred_element_type=F32)
             out = out + jnp.dot(mlp_ref[n], wv[:, cols], preferred_element_type=F32)
             b["part"][n, :, :, :, :, :, cols] = out.reshape(NZ, 2, 2, 2, ROWS, tile).astype(BF16)
             return 0
 
-        lax.fori_loop(0, width // tile, mul, 0)
+        lax.fori_loop(0, per, mul, 0)
 
     def finalize(n, rows):
         resid = x_ref[n].astype(F32) + rows.astype(BF16).astype(F32)
@@ -375,59 +411,63 @@
     def send_line(n, k):
         return remote(r4.at[n, place.z], r4.at[n, place.z], st_s.at[n, 8 + k], st_r.at[n, 8 + k], place.zpeer(k))
 
-    def consume(n):
-        if n == 0:
+    def pack(ref, top, den, hit):
+        for i, value in enumerate((top, den, hit)):
+            ref[2 * i:2 * i + 1, :] = value[:, :LANES]
+            ref[2 * i + 1:2 * i + 2, :] = value[:, LANES:]
+
+    def consume(n, j):
+        if n == BACK_FIRST and j == 0:
             load_e.wait()
-        tile = 512
+        tile = vocab_dev // 3
+        logits = dot_nt(emb[j * tile:(j + 1) * tile, :], b["rows"][n]) * scale
         nxt = next_ref[n:n + 1, :] - vocab_start
-
-        def mul(i, carry):
-            top, den, hit = carry
-            rows = pl.ds(pl.multiple_of(i * tile, tile), tile)
-            logits = dot_nt(emb[rows, :], b["rows"][...]) * scale
-            new = jnp.maximum(top, jnp.max(logits, axis=0, keepdims=True))
-            den = den * jnp.exp(top - new) + jnp.sum(jnp.exp(logits - new), axis=0, keepdims=True)
-            ids = lax.broadcasted_iota(jnp.int32, (tile, total), 0) + i * tile
-            hit = hit + jnp.sum(jnp.where(ids == nxt, logits, 0.0), axis=0, keepdims=True)
-            return new, den, hit
-
-        zero = jnp.zeros((1, total), F32)
-        top, den, hit = lax.fori_loop(0, vocab_dev // tile, mul, (jnp.full((1, total), -jnp.inf, F32), zero, zero))
-        r8[n, plane, 0:1, :] = top
-        r8[n, plane, 1:2, :] = den
-        r8[n, plane, 2:3, :] = hit
+        ids = lax.broadcasted_iota(jnp.int32, (tile, total), 0) + j * tile
+        top = jnp.max(logits, axis=0, keepdims=True)
+        hit = jnp.sum(jnp.where(ids == nxt, logits, 0.0), axis=0, keepdims=True)
+        if j > 0:
+            was, den = run[n, 0:1, :], run[n, 1:2, :]
+            top = jnp.maximum(was, top)
+            hit = run[n, 2:3, :] + hit
+        more = jnp.sum(jnp.exp(logits - top), axis=0, keepdims=True)
+        den = den * jnp.exp(was - top) + more if j > 0 else more
+        if j < 2:
+            run[n, 0:1, :] = top
+            run[n, 1:2, :] = den
+            run[n, 2:3, :] = hit
+            return
+        pack(r8.at[n, plane], top, den, hit)
         for k in range(1, 8):
             send_plane(n, k).start()
 
     def merge(buf, n, count):
-        top = buf[n, 0, 0:1, :]
+        top = buf[n, 0, 0:2, :]
         for i in range(1, count):
-            top = jnp.maximum(top, buf[n, i, 0:1, :])
+            top = jnp.maximum(top, buf[n, i, 0:2, :])
         den = jnp.zeros_like(top)
         hit = jnp.zeros_like(top)
         for i in range(count):
-            den = den + buf[n, i, 1:2, :] * jnp.exp(buf[n, i, 0:1, :] - top)
-            hit = hit + buf[n, i, 2:3, :]
+            den = den + buf[n, i, 2:4, :] * jnp.exp(buf[n, i, 0:2, :] - top)
+            hit = hit + buf[n, i, 4:6, :]
         return top, den, hit
 
-    run_exchange(place, b, width, BACK_ORDER, produce, lambda: None, finalize, consume)
-    last = [int(item[1]) for item in BACK_ORDER if item[0] == "g" and item[2] == "4"]
-    for n in last:
-        with jax.named_scope("plane"):
+    def after(n, j):
+        if j == 0:
             for k in range(1, 8):
                 send_plane(n, k).wait_recv()
             top, den, hit = merge(r8, n, 8)
-            r4[n, place.z, 0:1, :] = top
-            r4[n, place.z, 1:2, :] = den
-            r4[n, place.z, 2:3, :] = hit
+            r4[n, place.z, 0:2, :] = top
+            r4[n, place.z, 2:4, :] = den
+            r4[n, place.z, 4:6, :] = hit
             for k in range(1, NZ):
                 send_line(n, k).start()
-    for n in last:
-        with jax.named_scope("line"):
+        else:
             for k in range(1, NZ):
                 send_line(n, k).wait_recv()
             top, den, hit = merge(r4, n, NZ)
-            out_ref[n:n + 1, :] = hit - top - jnp.log(den)
+            out_ref[2 * n:2 * n + 2, :] = hit - top - jnp.log(den)
+
+    run_exchange(place, b, width, BACK_ORDER, produce, lambda: None, finalize, consume, after)
     for n in range(PIECES):
         for k in range(1, 8):
             send_plane(n, k).wait_send()
@@ -612,7 +652,7 @@
         next_rows = next_ids.reshape(pair_dims).transpose(0, 2, 1, 3).reshape(PIECES, piece_rows)
         log_probs = pl.pallas_call(
             functools.partial(back_kernel, vocab_dev, width, attn_dev, ff_dev, width ** -0.5),
-            out_shape=jax.ShapeDtypeStruct((PIECES, piece_rows), F32),
+            out_shape=jax.ShapeDtypeStruct((2 * PIECES, LANES), F32),
             in_specs=[vmem, vmem, vmem, vmem, vmem, anym, anym],
             out_specs=vmem,
             scratch_shapes=[
@@ -620,8 +660,9 @@
                 pltpu.VMEM((2 * attn_dev, width), BF16),
                 pltpu.VMEM((ff_dev, width), BF16),
                 pltpu.VMEM((NDEV, batch_dev, LANES), BF16),
-                pltpu.VMEM((PIECES, 8, 8, piece_rows), F32),
-                pltpu.VMEM((PIECES, NZ, 8, piece_rows), F32),
+                pltpu.VMEM((PIECES, 8, piece_rows), F32),
+                pltpu.VMEM((PIECES, 8, 8, LANES), F32),
+                pltpu.VMEM((PIECES, NZ, 8, LANES), F32),
                 dma((4,)),
                 dma((NDEV,)),
                 dma((NDEV,)),

time: 162 us -> 155 us (0.957)
  Pallas kernels: 157 us -> 150 us
    pallas_call x1, Pallas kernels: 67.5 us -> 62.4 us  [device_fn(): pl.pallas_call(functools.partial(front_kernel, vocab_dev, width, qkv_dev,...]
where the time goes in v4:
time: 155 us
  Pallas kernels  150 us (97%)
  local copies, waits for them, and re-layouts  3.23 us (2%)
    pallas_call x1, Pallas kernels, device_fn(): pl.pallas_call(functools.partial(back_kernel, vocab_dev, width, attn_dev,...  73.5 us
    pallas_call x1, Pallas kernels, device_fn(): pl.pallas_call(functools.partial(front_kernel, vocab_dev, width, qkv_dev,...  62.4 us
    pallas_call x1, Pallas kernels, device_fn(): pl.pallas_call(functools.partial(attention_kernel, heads, qkv_dev), out_s...  14.5 us

profile of v4, /device:TPU:0, one launch (start us, length us, event | category | flops | bytes accessed | tf_op | source)
XLA Modules:
  0.0 155.2 jit_solution(5857029412114129975)
XLA Ops:
  0.6 0.8 dynamic_slice.3.lens_ref
  1.4 0.0 copy-start.1
  1.4 0.1 convert_element_type.12
  1.5 0.1 compare_select_fusion
  1.6 0.8 fusion
  2.3 62.4 %front.1 = (bf16[4,8,2048]{2,1,0:T(8,128)(2,1)}, bf16[32,4,8,128]{3,2,1,0:T(8,128)(2,1)}, bf16[4,256,256]{2,1,0:T(8,128)(2,1)}) custom-call(s32[2,512]{1,0:T(2,128)} %tok_ref.1, bf16[2048]{0:T(1024)(128)(2,1)} %gain_ref.2, bf16[1536,2048]{1,0:T(8,128)(2,1)} %embed_ref.3, bf16[584,2048]{1,0:T(8,128)(2,1)} %bitcast.7), custom_call_target="tpu_custom_call" | custom-call | flops 40000000000 | bytes 8000000 | tf_op jit(solution)/shard_map/front/pallas_call | solution.py:594
  64.7 0.0 copy-done.1
  64.7 0.0 copy-start
  64.7 14.5 %attention.1 = (bf16[32,16,128]{2,1,0:T(8,128)(2,1)}, bf16[16,2048,128]{2,1,0:T(8,128)(2,1)}, bf16[16,2048,128]{2,1,0:T(8,128)(2,1)}) custom-call(s32[16]{0:T(128)} %copy-done.1, bf16[32,4,8,128]{3,2,1,0:T(8,128)(2,1)} %get-tuple-element.9.qkv_ref, f32[32,128]{1,0:T(8,128)} %get-tuple-element.16.cos_ref, f32[32,128]{1,0:T(8,128)} %get-tuple-element.15.sin_ref, ...), custom_call_target="tpu_custom_call" | custom-call | flops 1000000000 | bytes 34000000 | tf_op jit(solution)/shard_map/attention/pallas_call | solution.py:628
  79.3 0.0 copy-done
  79.3 0.2 reshape.42
  79.5 0.7 reshape.43.next_ref
  80.1 73.5 %back.1 = f32[8,128]{1,0:T(8,128)} custom-call(bf16[32,16,128]{2,1,0:T(8,128)(2,1)} %get-tuple-element.10.send_ref, bf16[4,256,256]{2,1,0:T(8,128)(2,1)} %get-tuple-element.11.mlp_ref, bf16[4,8,2048]{2,1,0:T(8,128)(2,1)} %get-tuple-element.12.x_ref, bf16[2048]{0:T(1024)(128)(2,1)} %gain_ref.3, s32[4,256]{1,0:T(4,128)} %reshape.43.next_ref, ...), custom_call_target="tpu_custom_call" | custom-call | flops 40000000000 | bytes 8000000 | tf_op jit(solution)/shard_map/back/pallas_call | solution.py:653
  153.6 0.7 reshape.44
  154.4 0.1 copy.16
  154.4 0.7 reshape.45
  (3 shorter events, 0.0 us)
Async XLA Ops:
  1.4 63.3 %copy-start.1 = (s32[16]{0:T(128)}, s32[16]{0:T(128)S(1)}, u32[]{:S(2)}) copy-start(s32[16]{0:T(128)S(1)} %dynamic_slice.3.lens_ref) | copy-start | bytes 196
  64.7 14.5 %copy-start = (s32[2,512]{1,0:T(2,128)S(1)}, s32[2,512]{1,0:T(2,128)}, u32[]{:S(2)}) copy-start(s32[2,512]{1,0:T(2,128)} %param.11) | copy-start | bytes 12292
